TPU v7x, 8 devices: a whole 2x2x1 slice. The times are simulated.
8 devices in a mesh: col: 4 (over z, y, x), row: 2 (over core).
Axes of the slice: x: 2, y: 2, z: 1, core: 2. Of those that a mesh axis runs over, the one named last changes fastest.
Arguments:
- f_rhs: float32 [64, 128, 512], P('row', 'col')
- u_init: float32 [64, 128, 512], P('row', 'col')
- kappa_cell: float32 [64, 128], P('row', 'col')
- solve_mats: bfloat16 [2, 4, 1024, 1600], P('row', 'col')
- omega_relax: float32 [], replicated
Outputs:
- output: float32 [64, 128, 512], P('row', 'col')
All inputs are finite; a program needn't handle non-finite values.
Results may differ from a plain program's by a relative error of at most 0.00175602.
Values are sent between devices in bfloat16 or wider.
A program may use at most 1 GiB of HBM per device.

v0:
```python
import math
import jax
import jax.numpy as jnp
from jax import lax
from jax.sharding import PartitionSpec as P

SWEEPS = 6


def shift_from(values, axis_name, axis_size, from_prev):
    if from_prev:
        pair_list = [(i, i + 1) for i in range(axis_size - 1)]
    else:
        pair_list = [(i + 1, i) for i in range(axis_size - 1)]
    return lax.ppermute(values, axis_name, pair_list)


def local_faces(kappa_blk, row_count, col_count):
    from_above = shift_from(kappa_blk[-1:, :], 'row', row_count, True)
    from_below = shift_from(kappa_blk[:1, :], 'row', row_count, False)
    from_left = shift_from(kappa_blk[:, -1:], 'col', col_count, True)
    from_right = shift_from(kappa_blk[:, :1], 'col', col_count, False)
    row_pos = lax.axis_index('row')
    col_pos = lax.axis_index('col')
    inner_v = 0.5 * (kappa_blk[1:, :] + kappa_blk[:-1, :])
    inner_h = 0.5 * (kappa_blk[:, 1:] + kappa_blk[:, :-1])
    edge_n = jnp.where(row_pos == 0, kappa_blk[:1, :], 0.5 * (kappa_blk[:1, :] + from_above))
    edge_s = jnp.where(row_pos == row_count - 1, kappa_blk[-1:, :], 0.5 * (from_below + kappa_blk[-1:, :]))
    edge_w = jnp.where(col_pos == 0, kappa_blk[:, :1], 0.5 * (kappa_blk[:, :1] + from_left))
    edge_e = jnp.where(col_pos == col_count - 1, kappa_blk[:, -1:], 0.5 * (from_right + kappa_blk[:, -1:]))
    face_n = jnp.concatenate([edge_n, inner_v], axis=0)
    face_s = jnp.concatenate([inner_v, edge_s], axis=0)
    face_w = jnp.concatenate([edge_w, inner_h], axis=1)
    face_e = jnp.concatenate([inner_h, edge_e], axis=1)
    return face_n, face_s, face_w, face_e


def apply_local(values, face_set, row_count, col_count):
    face_n, face_s, face_w, face_e = face_set
    from_above = shift_from(values[-1:], 'row', row_count, True).astype(jnp.float32)
    from_below = shift_from(values[:1], 'row', row_count, False).astype(jnp.float32)
    from_left = shift_from(values[:, -1:], 'col', col_count, True).astype(jnp.float32)
    from_right = shift_from(values[:, :1], 'col', col_count, False).astype(jnp.float32)
    center = values.astype(jnp.float32)
    up_nb = jnp.concatenate([from_above, center[:-1]], axis=0)
    down_nb = jnp.concatenate([center[1:], from_below], axis=0)
    left_nb = jnp.concatenate([from_left, center[:, :-1]], axis=1)
    right_nb = jnp.concatenate([center[:, 1:], from_right], axis=1)
    diag_sum = (face_n + face_s + face_w + face_e)[:, :, None]
    return (diag_sum * center
            - face_n[:, :, None] * up_nb
            - face_s[:, :, None] * down_nb
            - face_w[:, :, None] * left_nb
            - face_e[:, :, None] * right_nb)


def extend_block(res_bf, halo_depth, row_count, col_count):
    top_strip = shift_from(res_bf[-halo_depth:], 'row', row_count, True)
    bottom_strip = shift_from(res_bf[:halo_depth], 'row', row_count, False)
    tall_ext = jnp.concatenate([top_strip, res_bf, bottom_strip], axis=0)
    left_strip = shift_from(tall_ext[:, -halo_depth:], 'col', col_count, True)
    right_strip = shift_from(tall_ext[:, :halo_depth], 'col', col_count, False)
    return jnp.concatenate([left_strip, tall_ext, right_strip], axis=1)


def solution(mesh):
    row_count = mesh.shape['row']
    col_count = mesh.shape['col']
    grid_spec = P('row', 'col', None)

    def device_fn(f_blk, u_blk, kappa_blk, mat_blk, omega_relax):
        sub_size = u_blk.shape[0]
        rhs_count = u_blk.shape[2]
        ext_cells = mat_blk.shape[3]
        ext_size = math.isqrt(ext_cells)
        halo_depth = (ext_size - sub_size) // 2
        solve_mat = mat_blk[0, 0]
        face_set = local_faces(kappa_blk, row_count, col_count)
        residual = f_blk - apply_local(u_blk, face_set, row_count, col_count)
        u_cur = u_blk
        for sweep_idx in range(SWEEPS):
            ext_block = extend_block(residual.astype(jnp.bfloat16), halo_depth, row_count, col_count)
            local_z = jnp.dot(solve_mat, ext_block.reshape(ext_cells, rhs_count), preferred_element_type=jnp.float32)
            corr_bf = local_z.astype(jnp.bfloat16).reshape(sub_size, sub_size, rhs_count)
            u_cur = u_cur + omega_relax * corr_bf.astype(jnp.float32)
            if sweep_idx < SWEEPS - 1:
                residual = residual - omega_relax * apply_local(corr_bf, face_set, row_count, col_count)
        return u_cur

    return jax.shard_map(device_fn, mesh=mesh,
                         in_specs=(grid_spec, grid_spec, P('row', 'col'), P('row', 'col', None, None), P()),
                         out_specs=grid_spec, check_vma=False)
```

profile of v0, /device:TPU:0, one launch (start us, length us, event | category | flops | bytes accessed | tf_op | source)
XLA Modules:
  0.0 253.9 jit_solution(13181602080861850358)
XLA Ops:
  2.3 3.0 %collective-permute-start = (f32[1,32]{1,0:T(1,128)S(1)}, f32[1,32]{1,0:T(1,128)S(1)}, u32[]{:S(2)}, u32[]{:S(2)}) collective-permute-start(f32[1,32]{1,0:T(1,128)S(1)} %get-tuple-element.99), channel_id=1, source_target_pairs={{0,1},{2,3},{4,5},{6,7}} | collective-permute-start | bytes 392 | tf_op jit(solution)/shard_map/ppermute | solution.py:15
  7.5 5.9 %collective-permute-start.2 = (f32[32,1]{1,0:T(8,128)S(1)}, f32[32,1]{1,0:T(8,128)S(1)}, u32[]{:S(2)}, u32[]{:S(2)}) collective-permute-start(f32[32,1]{1,0:T(8,128)S(1)} %get-tuple-element.95), channel_id=1, source_target_pairs={{0,2},{2,4},{4,6},{1,3},{3,5},{5,7}} | collective-permute-start | bytes 392 | tf_op jit(solution)/shard_map/ppermute | solution.py:15
  13.4 1.9 fusion.80
  15.3 4.8 %collective-permute-start.6 = (f32[32,1,512]{2,1,0:T(1,128)}, f32[32,1,512]{2,1,0:T(1,128)S(1)}, u32[]{:S(2)}, u32[]{:S(2)}) collective-permute-start(f32[32,1,512]{2,1,0:T(1,128)} %get-tuple-element.24), channel_id=1, source_target_pairs={{0,2},{2,4},{4,6},{1,3},{3,5},{5,7}} | collective-permute-start | bytes 196616 | tf_op jit(solution)/shard_map/ppermute | solution.py:15
  23.3 5.1 %fusion.79 = (f32[31,32,512]{2,1,0:T(8,128)}, f32[31,32,512]{2,1,0:T(8,128)}) fusion(f32[32,32,512]{2,1,0:T(8,128)} %param.6), kind=kLoop, calls=%fused_computation.131 | loop fusion | bytes 8126464 | tf_op jit(solution)/shard_map/slice | solution.py:45
  28.4 2.5 fusion.81
  35.0 2.0 collective-permute-done.7
  37.0 6.7 %fusion.76 = (bf16[32,32,512]{2,1,0:T(8,128)(2,1)S(1)}, f32[32,32,512]{2,1,0:T(8,128)}) fusion(f32[32,32,512]{2,1,0:T(8,128)} %param.5, f32[32,1,512]{2,1,0:T(1,128)S(1)} %collective-permute-done.7, f32[32,31,512]{2,1,0:T(8,128)} %get-tuple-element.27, f32[32,32]{1,0:T(8,128)S(1)} %get-tuple-element.19, f32[32,31,512]{2,1,0:T(8,128)} %get-tuple-element.26, ...), kind=kLoop, calls=%fused_computation.129 | loop fusion | flops 7864320 | bytes 15749120 | tf_op jit(solution)/shard_map/convert_element_type | solution.py:82
  46.7 1.9 collective-permute-done.9
  49.5 5.2 %collective-permute-start.10 = (bf16[40,4,512]{2,1,0:T(4,128)(2,1)}, bf16[40,4,512]{2,1,0:T(4,128)(2,1)}, u32[]{:S(2)}, u32[]{:S(2)}) collective-permute-start(bf16[40,4,512]{2,1,0:T(4,128)(2,1)} %get-tuple-element.38), channel_id=1, source_target_pairs={{0,2},{2,4},{4,6},{1,3},{3,5},{5,7}} | collective-permute-start | bytes 491528 | tf_op jit(solution)/shard_map/ppermute | solution.py:15
  57.8 5.6 %collective-permute-done.11 = bf16[40,4,512]{2,1,0:T(4,128)(2,1)} collective-permute-done((bf16[40,4,512]{2,1,0:T(4,128)(2,1)}, bf16[40,4,512]{2,1,0:T(4,128)(2,1)}, u32[]{:S(2)}, u32[]{:S(2)}) %collective-permute-start.11) | collective-permute-done | bytes 163872 | tf_op jit(solution)/shard_map/ppermute | solution.py:15
  63.4 2.3 pad_maximum_fusion
  65.7 2.1 fusion.48
  71.1 3.2 %collective-permute-start.14 = (bf16[32,1,512]{2,1,0:T(2,128)(2,1)S(1)}, bf16[32,1,512]{2,1,0:T(2,128)(2,1)S(1)}, u32[]{:S(2)}, u32[]{:S(2)}) collective-permute-start(bf16[32,1,512]{2,1,0:T(2,128)(2,1)S(1)} %get-tuple-element.86), channel_id=1, source_target_pairs={{0,2},{2,4},{4,6},{1,3},{3,5},{5,7}} | collective-permute-start | bytes 98312 | tf_op jit(solution)/shard_map/ppermute | solution.py:15
  76.7 4.5 %collective-permute-done.15 = bf16[32,1,512]{2,1,0:T(2,128)(2,1)S(1)} collective-permute-done((bf16[32,1,512]{2,1,0:T(2,128)(2,1)S(1)}, bf16[32,1,512]{2,1,0:T(2,128)(2,1)S(1)}, u32[]{:S(2)}, u32[]{:S(2)}) %collective-permute-start.15) | collective-permute-done | bytes 32800 | tf_op jit(solution)/shard_map/ppermute | solution.py:15
  86.2 1.9 collective-permute-done.17
  88.3 3.0 %collective-permute-start.18 = (bf16[40,4,512]{2,1,0:T(4,128)(2,1)S(1)}, bf16[40,4,512]{2,1,0:T(4,128)(2,1)S(1)}, u32[]{:S(2)}, u32[]{:S(2)}) collective-permute-start(bf16[40,4,512]{2,1,0:T(4,128)(2,1)S(1)} %get-tuple-element.36), channel_id=1, source_target_pairs={{0,2},{2,4},{4,6},{1,3},{3,5},{5,7}} | collective-permute-start | bytes 491528 | tf_op jit(solution)/shard_map/ppermute | solution.py:15
  92.6 2.4 collective-permute-done.18
  95.0 4.5 %collective-permute-done.19 = bf16[40,4,512]{2,1,0:T(4,128)(2,1)S(1)} collective-permute-done((bf16[40,4,512]{2,1,0:T(4,128)(2,1)S(1)}, bf16[40,4,512]{2,1,0:T(4,128)(2,1)S(1)}, u32[]{:S(2)}, u32[]{:S(2)}) %collective-permute-start.19) | collective-permute-done | bytes 163872 | tf_op jit(solution)/shard_map/ppermute | solution.py:15
  100.5 2.1 fusion.51
  105.9 3.0 %collective-permute-start.22 = (bf16[32,1,512]{2,1,0:T(2,128)(2,1)S(1)}, bf16[32,1,512]{2,1,0:T(2,128)(2,1)S(1)}, u32[]{:S(2)}, u32[]{:S(2)}) collective-permute-start(bf16[32,1,512]{2,1,0:T(2,128)(2,1)S(1)} %get-tuple-element.76), channel_id=1, source_target_pairs={{0,2},{2,4},{4,6},{1,3},{3,5},{5,7}} | collective-permute-start | bytes 98312 | tf_op jit(solution)/shard_map/ppermute | solution.py:15
  111.3 4.4 %collective-permute-done.23 = bf16[32,1,512]{2,1,0:T(2,128)(2,1)S(1)} collective-permute-done((bf16[32,1,512]{2,1,0:T(2,128)(2,1)S(1)}, bf16[32,1,512]{2,1,0:T(2,128)(2,1)S(1)}, u32[]{:S(2)}, u32[]{:S(2)}) %collective-permute-start.23) | collective-permute-done | bytes 32800 | tf_op jit(solution)/shard_map/ppermute | solution.py:15
  120.7 1.9 collective-permute-done.25
  122.7 3.0 %collective-permute-start.26 = (bf16[40,4,512]{2,1,0:T(4,128)(2,1)S(1)}, bf16[40,4,512]{2,1,0:T(4,128)(2,1)S(1)}, u32[]{:S(2)}, u32[]{:S(2)}) collective-permute-start(bf16[40,4,512]{2,1,0:T(4,128)(2,1)S(1)} %get-tuple-element.34), channel_id=1, source_target_pairs={{0,2},{2,4},{4,6},{1,3},{3,5},{5,7}} | collective-permute-start | bytes 491528 | tf_op jit(solution)/shard_map/ppermute | solution.py:15
  127.0 2.4 collective-permute-done.26
  129.4 4.5 %collective-permute-done.27 = bf16[40,4,512]{2,1,0:T(4,128)(2,1)S(1)} collective-permute-done((bf16[40,4,512]{2,1,0:T(4,128)(2,1)S(1)}, bf16[40,4,512]{2,1,0:T(4,128)(2,1)S(1)}, u32[]{:S(2)}, u32[]{:S(2)}) %collective-permute-start.27) | collective-permute-done | bytes 163872 | tf_op jit(solution)/shard_map/ppermute | solution.py:15
  134.9 2.1 fusion.54
  140.3 3.0 %collective-permute-start.30 = (bf16[32,1,512]{2,1,0:T(2,128)(2,1)S(1)}, bf16[32,1,512]{2,1,0:T(2,128)(2,1)S(1)}, u32[]{:S(2)}, u32[]{:S(2)}) collective-permute-start(bf16[32,1,512]{2,1,0:T(2,128)(2,1)S(1)} %get-tuple-element.66), channel_id=1, source_target_pairs={{0,2},{2,4},{4,6},{1,3},{3,5},{5,7}} | collective-permute-start | bytes 98312 | tf_op jit(solution)/shard_map/ppermute | solution.py:15
  145.7 4.4 %collective-permute-done.31 = bf16[32,1,512]{2,1,0:T(2,128)(2,1)S(1)} collective-permute-done((bf16[32,1,512]{2,1,0:T(2,128)(2,1)S(1)}, bf16[32,1,512]{2,1,0:T(2,128)(2,1)S(1)}, u32[]{:S(2)}, u32[]{:S(2)}) %collective-permute-start.31) | collective-permute-done | bytes 32800 | tf_op jit(solution)/shard_map/ppermute | solution.py:15
  155.1 1.9 collective-permute-done.33
  157.2 3.0 %collective-permute-start.34 = (bf16[40,4,512]{2,1,0:T(4,128)(2,1)S(1)}, bf16[40,4,512]{2,1,0:T(4,128)(2,1)S(1)}, u32[]{:S(2)}, u32[]{:S(2)}) collective-permute-start(bf16[40,4,512]{2,1,0:T(4,128)(2,1)S(1)} %get-tuple-element.32), channel_id=1, source_target_pairs={{0,2},{2,4},{4,6},{1,3},{3,5},{5,7}} | collective-permute-start | bytes 491528 | tf_op jit(solution)/shard_map/ppermute | solution.py:15
  161.4 2.4 collective-permute-done.34
  163.9 4.5 %collective-permute-done.35 = bf16[40,4,512]{2,1,0:T(4,128)(2,1)S(1)} collective-permute-done((bf16[40,4,512]{2,1,0:T(4,128)(2,1)S(1)}, bf16[40,4,512]{2,1,0:T(4,128)(2,1)S(1)}, u32[]{:S(2)}, u32[]{:S(2)}) %collective-permute-start.35) | collective-permute-done | bytes 163872 | tf_op jit(solution)/shard_map/ppermute | solution.py:15
  169.4 2.1 fusion.57
  174.8 3.0 %collective-permute-start.38 = (bf16[32,1,512]{2,1,0:T(2,128)(2,1)S(1)}, bf16[32,1,512]{2,1,0:T(2,128)(2,1)S(1)}, u32[]{:S(2)}, u32[]{:S(2)}) collective-permute-start(bf16[32,1,512]{2,1,0:T(2,128)(2,1)S(1)} %get-tuple-element.56), channel_id=1, source_target_pairs={{0,2},{2,4},{4,6},{1,3},{3,5},{5,7}} | collective-permute-start | bytes 98312 | tf_op jit(solution)/shard_map/ppermute | solution.py:15
  180.2 4.4 %collective-permute-done.39 = bf16[32,1,512]{2,1,0:T(2,128)(2,1)S(1)} collective-permute-done((bf16[32,1,512]{2,1,0:T(2,128)(2,1)S(1)}, bf16[32,1,512]{2,1,0:T(2,128)(2,1)S(1)}, u32[]{:S(2)}, u32[]{:S(2)}) %collective-permute-start.39) | collective-permute-done | bytes 32800 | tf_op jit(solution)/shard_map/ppermute | solution.py:15
  191.6 3.0 %collective-permute-start.42 = (bf16[40,4,512]{2,1,0:T(4,128)(2,1)S(1)}, bf16[40,4,512]{2,1,0:T(4,128)(2,1)S(1)}, u32[]{:S(2)}, u32[]{:S(2)}) collective-permute-start(bf16[40,4,512]{2,1,0:T(4,128)(2,1)S(1)} %get-tuple-element.30), channel_id=1, source_target_pairs={{0,2},{2,4},{4,6},{1,3},{3,5},{5,7}} | collective-permute-start | bytes 491528 | tf_op jit(solution)/shard_map/ppermute | solution.py:15
  196.1 2.2 collective-permute-done.42
  198.3 4.5 %collective-permute-done.43 = bf16[40,4,512]{2,1,0:T(4,128)(2,1)S(1)} collective-permute-done((bf16[40,4,512]{2,1,0:T(4,128)(2,1)S(1)}, bf16[40,4,512]{2,1,0:T(4,128)(2,1)S(1)}, u32[]{:S(2)}, u32[]{:S(2)}) %collective-permute-start.43) | collective-permute-done | bytes 163872 | tf_op jit(solution)/shard_map/ppermute | solution.py:15
  203.8 2.1 fusion.60
  207.9 3.0 %collective-permute-start.44 = (bf16[1,32,512]{2,1,0:T(8,128)(2,1)S(1)}, bf16[1,32,512]{2,1,0:T(8,128)(2,1)S(1)}, u32[]{:S(2)}, u32[]{:S(2)}) collective-permute-start(bf16[1,32,512]{2,1,0:T(8,128)(2,1)S(1)} %get-tuple-element.49), channel_id=1, source_target_pairs={{0,1},{2,3},{4,5},{6,7}} | collective-permute-start | bytes 98312 | tf_op jit(solution)/shard_map/ppermute | solution.py:15
  212.2 4.5 %collective-permute-start.46 = (bf16[32,1,512]{2,1,0:T(2,128)(2,1)S(1)}, bf16[32,1,512]{2,1,0:T(2,128)(2,1)S(1)}, u32[]{:S(2)}, u32[]{:S(2)}) collective-permute-start(bf16[32,1,512]{2,1,0:T(2,128)(2,1)S(1)} %get-tuple-element.45), channel_id=1, source_target_pairs={{0,2},{2,4},{4,6},{1,3},{3,5},{5,7}} | collective-permute-start | bytes 98312 | tf_op jit(solution)/shard_map/ppermute | solution.py:15
  225.4 4.3 %collective-permute-start.50 = (bf16[40,4,512]{2,1,0:T(4,128)(2,1)S(1)}, bf16[40,4,512]{2,1,0:T(4,128)(2,1)S(1)}, u32[]{:S(2)}, u32[]{:S(2)}) collective-permute-start(bf16[40,4,512]{2,1,0:T(4,128)(2,1)S(1)} %get-tuple-element.28), channel_id=1, source_target_pairs={{0,2},{2,4},{4,6},{1,3},{3,5},{5,7}} | collective-permute-start | bytes 491528 | tf_op jit(solution)/shard_map/ppermute | solution.py:15
  231.0 2.4 collective-permute-done.50
  233.4 6.9 %collective-permute-done.51 = bf16[40,4,512]{2,1,0:T(4,128)(2,1)S(1)} collective-permute-done((bf16[40,4,512]{2,1,0:T(4,128)(2,1)S(1)}, bf16[40,4,512]{2,1,0:T(4,128)(2,1)S(1)}, u32[]{:S(2)}, u32[]{:S(2)}) %collective-permute-start.51) | collective-permute-done | bytes 163872 | tf_op jit(solution)/shard_map/ppermute | solution.py:15
  241.2 3.4 %multiply_bitcast_fusion = f32[1024,512]{0,1:T(8,128)} fusion(bf16[1600,512]{1,0:T(8,128)(2,1)S(1)} %bitcast.113, bf16[1,1,1024,1600]{2,3,1,0:T(8,128)(2,1)S(1)} %copy-done, f32[]{:T(128)S(6)} %copy.59), kind=kOutput, calls=%fused_computation.72 | convolution fusion | flops 1679294464 | bytes 7012356 | tf_op jit(solution)/shard_map/dot_general | solution.py:83
  244.7 2.9 %copy.53 = f32[1024,512]{1,0:T(8,128)} copy(f32[1024,512]{0,1:T(8,128)} %multiply_bitcast_fusion) | data formatting | bytes 4194304 | tf_op jit(solution)/shard_map/mul | solution.py:85
  247.6 6.3 %add_add_fusion = f32[32,32,512]{2,1,0:T(8,128)} fusion(f32[32,32,512]{2,1,0:T(8,128)} %bitcast.107, f32[32,32,512]{2,1,0:T(8,128)} %param.6, bf16[32,32,512]{2,1,0:T(8,128)(2,1)} %bitcast.106, bf16[32,32,512]{2,1,0:T(8,128)(2,1)} %bitcast.100, bf16[32,32,512]{2,1,0:T(8,128)(2,1)} %bitcast.94, bf16[32,32,512]{2,1,0:T(8,128)(2,1)} %bitcast.88, ...), kind=kLoop, calls=%fused_computation.73 | loop fusion | flops 8388608 | bytes 11534340 | tf_op jit(solution)/shard_map/add | solution.py:85
  (161 shorter events, 85.7 us)
Async XLA Ops:
  0.9 30.0 %collective-permute-start.1 = (f32[1,32]{1,0:T(1,128)S(1)}, f32[1,32]{1,0:T(1,128)S(1)}, u32[]{:S(2)}, u32[]{:S(2)}) collective-permute-start(f32[1,32]{1,0:T(1,128)S(1)} %get-tuple-element.98), channel_id=1, source_target_pairs={{1,0},{3,2},{5,4},{7,6}} | collective-permute-start | bytes 392 | tf_op jit(solution)/shard_map/ppermute | solution.py:15
  2.3 29.9 %collective-permute-start = (f32[1,32]{1,0:T(1,128)S(1)}, f32[1,32]{1,0:T(1,128)S(1)}, u32[]{:S(2)}, u32[]{:S(2)}) collective-permute-start(f32[1,32]{1,0:T(1,128)S(1)} %get-tuple-element.99), channel_id=1, source_target_pairs={{0,1},{2,3},{4,5},{6,7}} | collective-permute-start | bytes 392 | tf_op jit(solution)/shard_map/ppermute | solution.py:15
  6.2 27.3 %collective-permute-start.3 = (f32[32,1]{1,0:T(8,128)S(1)}, f32[32,1]{1,0:T(8,128)S(1)}, u32[]{:S(2)}, u32[]{:S(2)}) collective-permute-start(f32[32,1]{1,0:T(8,128)S(1)} %get-tuple-element.94), channel_id=1, source_target_pairs={{2,0},{4,2},{6,4},{3,1},{5,3},{7,5}} | collective-permute-start | bytes 392 | tf_op jit(solution)/shard_map/ppermute | solution.py:15
  7.5 27.3 %collective-permute-start.2 = (f32[32,1]{1,0:T(8,128)S(1)}, f32[32,1]{1,0:T(8,128)S(1)}, u32[]{:S(2)}, u32[]{:S(2)}) collective-permute-start(f32[32,1]{1,0:T(8,128)S(1)} %get-tuple-element.95), channel_id=1, source_target_pairs={{0,2},{2,4},{4,6},{1,3},{3,5},{5,7}} | collective-permute-start | bytes 392 | tf_op jit(solution)/shard_map/ppermute | solution.py:15
  15.3 19.7 %collective-permute-start.6 = (f32[32,1,512]{2,1,0:T(1,128)}, f32[32,1,512]{2,1,0:T(1,128)S(1)}, u32[]{:S(2)}, u32[]{:S(2)}) collective-permute-start(f32[32,1,512]{2,1,0:T(1,128)} %get-tuple-element.24), channel_id=1, source_target_pairs={{0,2},{2,4},{4,6},{1,3},{3,5},{5,7}} | collective-permute-start | bytes 196616 | tf_op jit(solution)/shard_map/ppermute | solution.py:15
  30.9 6.1 %collective-permute-start.7 = (f32[32,1,512]{2,1,0:T(1,128)S(1)}, f32[32,1,512]{2,1,0:T(1,128)S(1)}, u32[]{:S(2)}, u32[]{:S(2)}) collective-permute-start(f32[32,1,512]{2,1,0:T(1,128)S(1)} %get-tuple-element.25), channel_id=1, source_target_pairs={{2,0},{4,2},{6,4},{3,1},{5,3},{7,5}} | collective-permute-start | bytes 196616 | tf_op jit(solution)/shard_map/ppermute | solution.py:15
  32.2 4.9 %collective-permute-start.4 = (f32[1,32,512]{2,1,0:T(8,128)}, f32[1,32,512]{2,1,0:T(8,128)S(1)}, u32[]{:S(2)}, u32[]{:S(2)}) collective-permute-start(f32[1,32,512]{2,1,0:T(8,128)} %get-tuple-element.20), channel_id=1, source_target_pairs={{0,1},{2,3},{4,5},{6,7}} | collective-permute-start | bytes 196616 | tf_op jit(solution)/shard_map/ppermute | solution.py:15
  33.5 3.5 %collective-permute-start.5 = (f32[1,32,512]{2,1,0:T(8,128)}, f32[1,32,512]{2,1,0:T(8,128)S(1)}, u32[]{:S(2)}, u32[]{:S(2)}) collective-permute-start(f32[1,32,512]{2,1,0:T(8,128)} %get-tuple-element.21), channel_id=1, source_target_pairs={{1,0},{3,2},{5,4},{7,6}} | collective-permute-start | bytes 196616 | tf_op jit(solution)/shard_map/ppermute | solution.py:15
  45.4 3.2 %collective-permute-start.9 = (bf16[4,32,512]{2,1,0:T(8,128)(2,1)S(1)}, bf16[4,32,512]{2,1,0:T(8,128)(2,1)S(1)}, u32[]{:S(2)}, u32[]{:S(2)}) collective-permute-start(bf16[4,32,512]{2,1,0:T(8,128)(2,1)S(1)} %get-tuple-element.91), channel_id=1, source_target_pairs={{1,0},{3,2},{5,4},{7,6}} | collective-permute-start | bytes 393224 | tf_op jit(solution)/shard_map/ppermute | solution.py:15
  49.5 8.3 %collective-permute-start.10 = (bf16[40,4,512]{2,1,0:T(4,128)(2,1)}, bf16[40,4,512]{2,1,0:T(4,128)(2,1)}, u32[]{:S(2)}, u32[]{:S(2)}) collective-permute-start(bf16[40,4,512]{2,1,0:T(4,128)(2,1)} %get-tuple-element.38), channel_id=1, source_target_pairs={{0,2},{2,4},{4,6},{1,3},{3,5},{5,7}} | collective-permute-start | bytes 491528 | tf_op jit(solution)/shard_map/ppermute | solution.py:15
  54.7 8.6 %collective-permute-start.11 = (bf16[40,4,512]{2,1,0:T(4,128)(2,1)}, bf16[40,4,512]{2,1,0:T(4,128)(2,1)}, u32[]{:S(2)}, u32[]{:S(2)}) collective-permute-start(bf16[40,4,512]{2,1,0:T(4,128)(2,1)} %get-tuple-element.39), channel_id=1, source_target_pairs={{2,0},{4,2},{6,4},{3,1},{5,3},{7,5}} | collective-permute-start | bytes 491528 | tf_op jit(solution)/shard_map/ppermute | solution.py:15
  68.5 7.8 %collective-permute-start.12 = (bf16[1,32,512]{2,1,0:T(8,128)(2,1)S(1)}, bf16[1,32,512]{2,1,0:T(8,128)(2,1)S(1)}, u32[]{:S(2)}, u32[]{:S(2)}) collective-permute-start(bf16[1,32,512]{2,1,0:T(8,128)(2,1)S(1)} %get-tuple-element.82), channel_id=1, source_target_pairs={{0,1},{2,3},{4,5},{6,7}} | collective-permute-start | bytes 98312 | tf_op jit(solution)/shard_map/ppermute | solution.py:15
  69.8 6.5 %collective-permute-start.13 = (bf16[1,32,512]{2,1,0:T(8,128)(2,1)S(1)}, bf16[1,32,512]{2,1,0:T(8,128)(2,1)S(1)}, u32[]{:S(2)}, u32[]{:S(2)}) collective-permute-start(bf16[1,32,512]{2,1,0:T(8,128)(2,1)S(1)} %get-tuple-element.83), channel_id=1, source_target_pairs={{1,0},{3,2},{5,4},{7,6}} | collective-permute-start | bytes 98312 | tf_op jit(solution)/shard_map/ppermute | solution.py:15
  71.1 5.5 %collective-permute-start.14 = (bf16[32,1,512]{2,1,0:T(2,128)(2,1)S(1)}, bf16[32,1,512]{2,1,0:T(2,128)(2,1)S(1)}, u32[]{:S(2)}, u32[]{:S(2)}) collective-permute-start(bf16[32,1,512]{2,1,0:T(2,128)(2,1)S(1)} %get-tuple-element.86), channel_id=1, source_target_pairs={{0,2},{2,4},{4,6},{1,3},{3,5},{5,7}} | collective-permute-start | bytes 98312 | tf_op jit(solution)/shard_map/ppermute | solution.py:15
  74.3 6.9 %collective-permute-start.15 = (bf16[32,1,512]{2,1,0:T(2,128)(2,1)S(1)}, bf16[32,1,512]{2,1,0:T(2,128)(2,1)S(1)}, u32[]{:S(2)}, u32[]{:S(2)}) collective-permute-start(bf16[32,1,512]{2,1,0:T(2,128)(2,1)S(1)} %get-tuple-element.87), channel_id=1, source_target_pairs={{2,0},{4,2},{6,4},{3,1},{5,3},{7,5}} | collective-permute-start | bytes 98312 | tf_op jit(solution)/shard_map/ppermute | solution.py:15
  83.0 3.2 %collective-permute-start.16 = (bf16[4,32,512]{2,1,0:T(8,128)(2,1)S(1)}, bf16[4,32,512]{2,1,0:T(8,128)(2,1)S(1)}, u32[]{:S(2)}, u32[]{:S(2)}) collective-permute-start(bf16[4,32,512]{2,1,0:T(8,128)(2,1)S(1)} %get-tuple-element.80), channel_id=1, source_target_pairs={{0,1},{2,3},{4,5},{6,7}} | collective-permute-start | bytes 393224 | tf_op jit(solution)/shard_map/ppermute | solution.py:15
  84.9 3.2 %collective-permute-start.17 = (bf16[4,32,512]{2,1,0:T(8,128)(2,1)S(1)}, bf16[4,32,512]{2,1,0:T(8,128)(2,1)S(1)}, u32[]{:S(2)}, u32[]{:S(2)}) collective-permute-start(bf16[4,32,512]{2,1,0:T(8,128)(2,1)S(1)} %get-tuple-element.81), channel_id=1, source_target_pairs={{1,0},{3,2},{5,4},{7,6}} | collective-permute-start | bytes 393224 | tf_op jit(solution)/shard_map/ppermute | solution.py:15
  88.3 6.7 %collective-permute-start.18 = (bf16[40,4,512]{2,1,0:T(4,128)(2,1)S(1)}, bf16[40,4,512]{2,1,0:T(4,128)(2,1)S(1)}, u32[]{:S(2)}, u32[]{:S(2)}) collective-permute-start(bf16[40,4,512]{2,1,0:T(4,128)(2,1)S(1)} %get-tuple-element.36), channel_id=1, source_target_pairs={{0,2},{2,4},{4,6},{1,3},{3,5},{5,7}} | collective-permute-start | bytes 491528 | tf_op jit(solution)/shard_map/ppermute | solution.py:15
  91.3 8.2 %collective-permute-start.19 = (bf16[40,4,512]{2,1,0:T(4,128)(2,1)S(1)}, bf16[40,4,512]{2,1,0:T(4,128)(2,1)S(1)}, u32[]{:S(2)}, u32[]{:S(2)}) collective-permute-start(bf16[40,4,512]{2,1,0:T(4,128)(2,1)S(1)} %get-tuple-element.37), channel_id=1, source_target_pairs={{2,0},{4,2},{6,4},{3,1},{5,3},{7,5}} | collective-permute-start | bytes 491528 | tf_op jit(solution)/shard_map/ppermute | solution.py:15
  103.3 7.7 %collective-permute-start.20 = (bf16[1,32,512]{2,1,0:T(8,128)(2,1)S(1)}, bf16[1,32,512]{2,1,0:T(8,128)(2,1)S(1)}, u32[]{:S(2)}, u32[]{:S(2)}) collective-permute-start(bf16[1,32,512]{2,1,0:T(8,128)(2,1)S(1)} %get-tuple-element.72), channel_id=1, source_target_pairs={{0,1},{2,3},{4,5},{6,7}} | collective-permute-start | bytes 98312 | tf_op jit(solution)/shard_map/ppermute | solution.py:15
  104.6 6.4 %collective-permute-start.21 = (bf16[1,32,512]{2,1,0:T(8,128)(2,1)S(1)}, bf16[1,32,512]{2,1,0:T(8,128)(2,1)S(1)}, u32[]{:S(2)}, u32[]{:S(2)}) collective-permute-start(bf16[1,32,512]{2,1,0:T(8,128)(2,1)S(1)} %get-tuple-element.73), channel_id=1, source_target_pairs={{1,0},{3,2},{5,4},{7,6}} | collective-permute-start | bytes 98312 | tf_op jit(solution)/shard_map/ppermute | solution.py:15
  105.9 5.3 %collective-permute-start.22 = (bf16[32,1,512]{2,1,0:T(2,128)(2,1)S(1)}, bf16[32,1,512]{2,1,0:T(2,128)(2,1)S(1)}, u32[]{:S(2)}, u32[]{:S(2)}) collective-permute-start(bf16[32,1,512]{2,1,0:T(2,128)(2,1)S(1)} %get-tuple-element.76), channel_id=1, source_target_pairs={{0,2},{2,4},{4,6},{1,3},{3,5},{5,7}} | collective-permute-start | bytes 98312 | tf_op jit(solution)/shard_map/ppermute | solution.py:15
  108.9 6.7 %collective-permute-start.23 = (bf16[32,1,512]{2,1,0:T(2,128)(2,1)S(1)}, bf16[32,1,512]{2,1,0:T(2,128)(2,1)S(1)}, u32[]{:S(2)}, u32[]{:S(2)}) collective-permute-start(bf16[32,1,512]{2,1,0:T(2,128)(2,1)S(1)} %get-tuple-element.77), channel_id=1, source_target_pairs={{2,0},{4,2},{6,4},{3,1},{5,3},{7,5}} | collective-permute-start | bytes 98312 | tf_op jit(solution)/shard_map/ppermute | solution.py:15
  119.3 3.2 %collective-permute-start.25 = (bf16[4,32,512]{2,1,0:T(8,128)(2,1)S(1)}, bf16[4,32,512]{2,1,0:T(8,128)(2,1)S(1)}, u32[]{:S(2)}, u32[]{:S(2)}) collective-permute-start(bf16[4,32,512]{2,1,0:T(8,128)(2,1)S(1)} %get-tuple-element.71), channel_id=1, source_target_pairs={{1,0},{3,2},{5,4},{7,6}} | collective-permute-start | bytes 393224 | tf_op jit(solution)/shard_map/ppermute | solution.py:15
  122.7 6.7 %collective-permute-start.26 = (bf16[40,4,512]{2,1,0:T(4,128)(2,1)S(1)}, bf16[40,4,512]{2,1,0:T(4,128)(2,1)S(1)}, u32[]{:S(2)}, u32[]{:S(2)}) collective-permute-start(bf16[40,4,512]{2,1,0:T(4,128)(2,1)S(1)} %get-tuple-element.34), channel_id=1, source_target_pairs={{0,2},{2,4},{4,6},{1,3},{3,5},{5,7}} | collective-permute-start | bytes 491528 | tf_op jit(solution)/shard_map/ppermute | solution.py:15
  125.7 8.2 %collective-permute-start.27 = (bf16[40,4,512]{2,1,0:T(4,128)(2,1)S(1)}, bf16[40,4,512]{2,1,0:T(4,128)(2,1)S(1)}, u32[]{:S(2)}, u32[]{:S(2)}) collective-permute-start(bf16[40,4,512]{2,1,0:T(4,128)(2,1)S(1)} %get-tuple-element.35), channel_id=1, source_target_pairs={{2,0},{4,2},{6,4},{3,1},{5,3},{7,5}} | collective-permute-start | bytes 491528 | tf_op jit(solution)/shard_map/ppermute | solution.py:15
  137.7 7.5 %collective-permute-start.28 = (bf16[1,32,512]{2,1,0:T(8,128)(2,1)S(1)}, bf16[1,32,512]{2,1,0:T(8,128)(2,1)S(1)}, u32[]{:S(2)}, u32[]{:S(2)}) collective-permute-start(bf16[1,32,512]{2,1,0:T(8,128)(2,1)S(1)} %get-tuple-element.62), channel_id=1, source_target_pairs={{0,1},{2,3},{4,5},{6,7}} | collective-permute-start | bytes 98312 | tf_op jit(solution)/shard_map/ppermute | solution.py:15
  139.0 6.2 %collective-permute-start.29 = (bf16[1,32,512]{2,1,0:T(8,128)(2,1)S(1)}, bf16[1,32,512]{2,1,0:T(8,128)(2,1)S(1)}, u32[]{:S(2)}, u32[]{:S(2)}) collective-permute-start(bf16[1,32,512]{2,1,0:T(8,128)(2,1)S(1)} %get-tuple-element.63), channel_id=1, source_target_pairs={{1,0},{3,2},{5,4},{7,6}} | collective-permute-start | bytes 98312 | tf_op jit(solution)/shard_map/ppermute | solution.py:15
  140.3 5.3 %collective-permute-start.30 = (bf16[32,1,512]{2,1,0:T(2,128)(2,1)S(1)}, bf16[32,1,512]{2,1,0:T(2,128)(2,1)S(1)}, u32[]{:S(2)}, u32[]{:S(2)}) collective-permute-start(bf16[32,1,512]{2,1,0:T(2,128)(2,1)S(1)} %get-tuple-element.66), channel_id=1, source_target_pairs={{0,2},{2,4},{4,6},{1,3},{3,5},{5,7}} | collective-permute-start | bytes 98312 | tf_op jit(solution)/shard_map/ppermute | solution.py:15
  143.3 6.7 %collective-permute-start.31 = (bf16[32,1,512]{2,1,0:T(2,128)(2,1)S(1)}, bf16[32,1,512]{2,1,0:T(2,128)(2,1)S(1)}, u32[]{:S(2)}, u32[]{:S(2)}) collective-permute-start(bf16[32,1,512]{2,1,0:T(2,128)(2,1)S(1)} %get-tuple-element.67), channel_id=1, source_target_pairs={{2,0},{4,2},{6,4},{3,1},{5,3},{7,5}} | collective-permute-start | bytes 98312 | tf_op jit(solution)/shard_map/ppermute | solution.py:15
  151.9 3.2 %collective-permute-start.32 = (bf16[4,32,512]{2,1,0:T(8,128)(2,1)S(1)}, bf16[4,32,512]{2,1,0:T(8,128)(2,1)S(1)}, u32[]{:S(2)}, u32[]{:S(2)}) collective-permute-start(bf16[4,32,512]{2,1,0:T(8,128)(2,1)S(1)} %get-tuple-element.60), channel_id=1, source_target_pairs={{0,1},{2,3},{4,5},{6,7}} | collective-permute-start | bytes 393224 | tf_op jit(solution)/shard_map/ppermute | solution.py:15
  153.8 3.2 %collective-permute-start.33 = (bf16[4,32,512]{2,1,0:T(8,128)(2,1)S(1)}, bf16[4,32,512]{2,1,0:T(8,128)(2,1)S(1)}, u32[]{:S(2)}, u32[]{:S(2)}) collective-permute-start(bf16[4,32,512]{2,1,0:T(8,128)(2,1)S(1)} %get-tuple-element.61), channel_id=1, source_target_pairs={{1,0},{3,2},{5,4},{7,6}} | collective-permute-start | bytes 393224 | tf_op jit(solution)/shard_map/ppermute | solution.py:15
  157.2 6.7 %collective-permute-start.34 = (bf16[40,4,512]{2,1,0:T(4,128)(2,1)S(1)}, bf16[40,4,512]{2,1,0:T(4,128)(2,1)S(1)}, u32[]{:S(2)}, u32[]{:S(2)}) collective-permute-start(bf16[40,4,512]{2,1,0:T(4,128)(2,1)S(1)} %get-tuple-element.32), channel_id=1, source_target_pairs={{0,2},{2,4},{4,6},{1,3},{3,5},{5,7}} | collective-permute-start | bytes 491528 | tf_op jit(solution)/shard_map/ppermute | solution.py:15
  160.1 8.2 %collective-permute-start.35 = (bf16[40,4,512]{2,1,0:T(4,128)(2,1)S(1)}, bf16[40,4,512]{2,1,0:T(4,128)(2,1)S(1)}, u32[]{:S(2)}, u32[]{:S(2)}) collective-permute-start(bf16[40,4,512]{2,1,0:T(4,128)(2,1)S(1)} %get-tuple-element.33), channel_id=1, source_target_pairs={{2,0},{4,2},{6,4},{3,1},{5,3},{7,5}} | collective-permute-start | bytes 491528 | tf_op jit(solution)/shard_map/ppermute | solution.py:15
  172.2 7.5 %collective-permute-start.36 = (bf16[1,32,512]{2,1,0:T(8,128)(2,1)S(1)}, bf16[1,32,512]{2,1,0:T(8,128)(2,1)S(1)}, u32[]{:S(2)}, u32[]{:S(2)}) collective-permute-start(bf16[1,32,512]{2,1,0:T(8,128)(2,1)S(1)} %get-tuple-element.52), channel_id=1, source_target_pairs={{0,1},{2,3},{4,5},{6,7}} | collective-permute-start | bytes 98312 | tf_op jit(solution)/shard_map/ppermute | solution.py:15
  173.5 6.2 %collective-permute-start.37 = (bf16[1,32,512]{2,1,0:T(8,128)(2,1)S(1)}, bf16[1,32,512]{2,1,0:T(8,128)(2,1)S(1)}, u32[]{:S(2)}, u32[]{:S(2)}) collective-permute-start(bf16[1,32,512]{2,1,0:T(8,128)(2,1)S(1)} %get-tuple-element.53), channel_id=1, source_target_pairs={{1,0},{3,2},{5,4},{7,6}} | collective-permute-start | bytes 98312 | tf_op jit(solution)/shard_map/ppermute | solution.py:15
  174.8 5.3 %collective-permute-start.38 = (bf16[32,1,512]{2,1,0:T(2,128)(2,1)S(1)}, bf16[32,1,512]{2,1,0:T(2,128)(2,1)S(1)}, u32[]{:S(2)}, u32[]{:S(2)}) collective-permute-start(bf16[32,1,512]{2,1,0:T(2,128)(2,1)S(1)} %get-tuple-element.56), channel_id=1, source_target_pairs={{0,2},{2,4},{4,6},{1,3},{3,5},{5,7}} | collective-permute-start | bytes 98312 | tf_op jit(solution)/shard_map/ppermute | solution.py:15
  177.8 6.7 %collective-permute-start.39 = (bf16[32,1,512]{2,1,0:T(2,128)(2,1)S(1)}, bf16[32,1,512]{2,1,0:T(2,128)(2,1)S(1)}, u32[]{:S(2)}, u32[]{:S(2)}) collective-permute-start(bf16[32,1,512]{2,1,0:T(2,128)(2,1)S(1)} %get-tuple-element.57), channel_id=1, source_target_pairs={{2,0},{4,2},{6,4},{3,1},{5,3},{7,5}} | collective-permute-start | bytes 98312 | tf_op jit(solution)/shard_map/ppermute | solution.py:15
  188.2 3.2 %collective-permute-start.41 = (bf16[4,32,512]{2,1,0:T(8,128)(2,1)S(1)}, bf16[4,32,512]{2,1,0:T(8,128)(2,1)S(1)}, u32[]{:S(2)}, u32[]{:S(2)}) collective-permute-start(bf16[4,32,512]{2,1,0:T(8,128)(2,1)S(1)} %get-tuple-element.51), channel_id=1, source_target_pairs={{1,0},{3,2},{5,4},{7,6}} | collective-permute-start | bytes 393224 | tf_op jit(solution)/shard_map/ppermute | solution.py:15
  191.6 6.7 %collective-permute-start.42 = (bf16[40,4,512]{2,1,0:T(4,128)(2,1)S(1)}, bf16[40,4,512]{2,1,0:T(4,128)(2,1)S(1)}, u32[]{:S(2)}, u32[]{:S(2)}) collective-permute-start(bf16[40,4,512]{2,1,0:T(4,128)(2,1)S(1)} %get-tuple-element.30), channel_id=1, source_target_pairs={{0,2},{2,4},{4,6},{1,3},{3,5},{5,7}} | collective-permute-start | bytes 491528 | tf_op jit(solution)/shard_map/ppermute | solution.py:15
  194.6 8.2 %collective-permute-start.43 = (bf16[40,4,512]{2,1,0:T(4,128)(2,1)S(1)}, bf16[40,4,512]{2,1,0:T(4,128)(2,1)S(1)}, u32[]{:S(2)}, u32[]{:S(2)}) collective-permute-start(bf16[40,4,512]{2,1,0:T(4,128)(2,1)S(1)} %get-tuple-element.31), channel_id=1, source_target_pairs={{2,0},{4,2},{6,4},{3,1},{5,3},{7,5}} | collective-permute-start | bytes 491528 | tf_op jit(solution)/shard_map/ppermute | solution.py:15
  206.6 10.8 %collective-permute-start.45 = (bf16[1,32,512]{2,1,0:T(8,128)(2,1)S(1)}, bf16[1,32,512]{2,1,0:T(8,128)(2,1)S(1)}, u32[]{:S(2)}, u32[]{:S(2)}) collective-permute-start(bf16[1,32,512]{2,1,0:T(8,128)(2,1)S(1)} %get-tuple-element.48), channel_id=1, source_target_pairs={{1,0},{3,2},{5,4},{7,6}} | collective-permute-start | bytes 98312 | tf_op jit(solution)/shard_map/ppermute | solution.py:15
  207.9 9.5 %collective-permute-start.44 = (bf16[1,32,512]{2,1,0:T(8,128)(2,1)S(1)}, bf16[1,32,512]{2,1,0:T(8,128)(2,1)S(1)}, u32[]{:S(2)}, u32[]{:S(2)}) collective-permute-start(bf16[1,32,512]{2,1,0:T(8,128)(2,1)S(1)} %get-tuple-element.49), channel_id=1, source_target_pairs={{0,1},{2,3},{4,5},{6,7}} | collective-permute-start | bytes 98312 | tf_op jit(solution)/shard_map/ppermute | solution.py:15
  210.9 6.5 %collective-permute-start.47 = (bf16[32,1,512]{2,1,0:T(2,128)(2,1)S(1)}, bf16[32,1,512]{2,1,0:T(2,128)(2,1)S(1)}, u32[]{:S(2)}, u32[]{:S(2)}) collective-permute-start(bf16[32,1,512]{2,1,0:T(2,128)(2,1)S(1)} %get-tuple-element.44), channel_id=1, source_target_pairs={{2,0},{4,2},{6,4},{3,1},{5,3},{7,5}} | collective-permute-start | bytes 98312 | tf_op jit(solution)/shard_map/ppermute | solution.py:15
  212.2 6.4 %collective-permute-start.46 = (bf16[32,1,512]{2,1,0:T(2,128)(2,1)S(1)}, bf16[32,1,512]{2,1,0:T(2,128)(2,1)S(1)}, u32[]{:S(2)}, u32[]{:S(2)}) collective-permute-start(bf16[32,1,512]{2,1,0:T(2,128)(2,1)S(1)} %get-tuple-element.45), channel_id=1, source_target_pairs={{0,2},{2,4},{4,6},{1,3},{3,5},{5,7}} | collective-permute-start | bytes 98312 | tf_op jit(solution)/shard_map/ppermute | solution.py:15
  222.0 3.2 %collective-permute-start.49 = (bf16[4,32,512]{2,1,0:T(8,128)(2,1)S(1)}, bf16[4,32,512]{2,1,0:T(8,128)(2,1)S(1)}, u32[]{:S(2)}, u32[]{:S(2)}) collective-permute-start(bf16[4,32,512]{2,1,0:T(8,128)(2,1)S(1)} %get-tuple-element.41), channel_id=1, source_target_pairs={{1,0},{3,2},{5,4},{7,6}} | collective-permute-start | bytes 393224 | tf_op jit(solution)/shard_map/ppermute | solution.py:15
  225.4 8.0 %collective-permute-start.50 = (bf16[40,4,512]{2,1,0:T(4,128)(2,1)S(1)}, bf16[40,4,512]{2,1,0:T(4,128)(2,1)S(1)}, u32[]{:S(2)}, u32[]{:S(2)}) collective-permute-start(bf16[40,4,512]{2,1,0:T(4,128)(2,1)S(1)} %get-tuple-element.28), channel_id=1, source_target_pairs={{0,2},{2,4},{4,6},{1,3},{3,5},{5,7}} | collective-permute-start | bytes 491528 | tf_op jit(solution)/shard_map/ppermute | solution.py:15
  229.7 10.6 %collective-permute-start.51 = (bf16[40,4,512]{2,1,0:T(4,128)(2,1)S(1)}, bf16[40,4,512]{2,1,0:T(4,128)(2,1)S(1)}, u32[]{:S(2)}, u32[]{:S(2)}) collective-permute-start(bf16[40,4,512]{2,1,0:T(4,128)(2,1)S(1)} %get-tuple-element.29), channel_id=1, source_target_pairs={{2,0},{4,2},{6,4},{3,1},{5,3},{7,5}} | collective-permute-start | bytes 491528 | tf_op jit(solution)/shard_map/ppermute | solution.py:15
  (15 other events, 166.4 us)
where the time goes:
time: 256 us; the launch traced here: 254 us
  starting transfers between devices  106 us (41%)
  waiting for transfers between devices  77.2 us (30%)
  other arithmetic  32.8 us (13%)
  local copies, waits for them, and re-layouts  21.9 us (9%)
  matrix products  14 us (5%)
    ppermute x52, starting transfers between devices, shift_from(): return lax.ppermute(values, axis_name, pair_list)  106 us
    ppermute x52, waiting for transfers between devices, shift_from(): return lax.ppermute(values, axis_name, pair_list)  77.2 us
    convert_element_type x6, other arithmetic, device_fn(): residual.astype(jnp.bfloat16)  15.2 us
    dot_general x6, matrix products, device_fn(): jnp.dot(solve_mat, ext_block.reshape(ext_cells, rhs_count), preferred_ele...  14 us
    slice x5, local copies, waits for them, and re-layouts, apply_local(): up_nb = jnp.concatenate([from_above, center[:-1]], axis=0)  7.29 us
    concatenate x6, other arithmetic, extend_block(): return jnp.concatenate([left_strip, tall_ext, right_strip], axis=1)  7.12 us
    add x1, other arithmetic, device_fn(): u_cur = u_cur + omega_relax * corr_bf.astype(jnp.float32)  6.29 us
  transfers between devices with their start and end apart: 52, of which 28 were waited for; matrix products, arithmetic and copies ran while one was open for 7% of the time, Pallas kernels for 0%

commit v1 on v0

v1 whole, which is shorter than its diff:
```python
import functools
import jax
import jax.numpy as jnp
from jax import lax
from jax.experimental import pallas as pl
from jax.experimental.pallas import tpu as pltpu
from jax.sharding import PartitionSpec as P

SWEEPS = 6
SUB = 32
MARGIN = 4
EXT = SUB + 2 * MARGIN
CELLS = SUB * SUB
LANES = 128
TILES = 2
GROUP = TILES * LANES
COLS_AT = CELLS
ROWS_AT = CELLS + 256
CORN_AT = ROWS_AT + 128
DEPTH = CORN_AT + 128
PAD = SUB
MESH = pl.DeviceIdType.MESH
F32 = jnp.float32
BF16 = jnp.bfloat16


def own_source(n):
    return ((n >> 5) + MARGIN) * EXT + (n & 31) + MARGIN


def side_column(side, dist):
    return jnp.where(side == 0, MARGIN - 1 - dist, MARGIN + SUB + dist)


def kernel(groups, col_count,
           f_hbm, u_hbm, kap_ref, mat_hbm, om_ref, out_ref,
           mat_v, mat_p, res, zf, u_v, e_v, kb, cd, cn, cs, cw, ce, cedge, crow,
           send_p, send_b, send_u, recv_p, recv_b, recv_u, zrow, kcol_s, kcol_r, krow_r,
           in_sem, mat_sem, sp_sem, rp_sem, sb_sem, rb_sem, su_sem, ru_sem,
           sz_sem, rz_sem, sf_sem, rf_sem, sk_sem, rk_sem):
    col = lax.axis_index('col')
    row = lax.axis_index('row')
    has = (col > 0, col < col_count - 1)
    side_dev = ((col - 1, row), (col + 1, row))
    partner = (col, 1 - row)
    brow = (SUB - 1) * (1 - row)
    om = om_ref[0]

    loads = []
    for g in range(groups):
        for t in range(TILES):
            k = g * TILES + t
            lanes = pl.ds(k * LANES, LANES)
            loads.append((
                pltpu.make_async_copy(u_hbm.at[:, lanes], zf.at[k, pl.ds(PAD, CELLS)], in_sem.at[0, k]),
                pltpu.make_async_copy(f_hbm.at[:, lanes], res.at[k], in_sem.at[1, k]),
                pltpu.make_async_copy(u_hbm.at[:, lanes], u_v.at[k], in_sem.at[2, k])))
    for a, b, c in loads:
        a.start()
        b.start()
    mat_copy = pltpu.make_async_copy(mat_hbm, mat_v, mat_sem)
    mat_copy.start()
    for a, b, c in loads:
        c.start()

    barrier = pltpu.get_barrier_semaphore()
    pl.semaphore_signal(barrier, inc=1, device_id=partner, device_id_type=MESH)
    for s in range(2):
        @pl.when(has[s])
        def _():
            pl.semaphore_signal(barrier, inc=1, device_id=side_dev[s], device_id_type=MESH)
    waits = 1 + has[0].astype(jnp.int32) + has[1].astype(jnp.int32)
    pl.semaphore_wait(barrier, waits)

    zero_row = jnp.zeros((SUB, LANES), F32)
    kap_t = jnp.transpose(jnp.concatenate([kap_ref[...], jnp.zeros((LANES - SUB, SUB), F32)], axis=0))
    kb[pl.ds(0, SUB)] = zero_row
    kb[pl.ds(PAD + CELLS, SUB)] = zero_row
    for r in range(SUB):
        kb[pl.ds(PAD + r * SUB, SUB)] = jnp.broadcast_to(kap_t[:, r:r + 1], (SUB, LANES))

    def kcol_copy(s):
        return pltpu.make_async_remote_copy(kcol_s.at[s], kcol_r.at[1 - s], sk_sem.at[s], rk_sem.at[1 - s],
                                            device_id=side_dev[s], device_id_type=MESH)

    def krow_copy():
        return pltpu.make_async_remote_copy(kb.at[pl.ds(PAD + brow * SUB, SUB)], krow_r, sk_sem.at[2], rk_sem.at[2],
                                            device_id=partner, device_id_type=MESH)

    edge_col = (0, SUB - 1)

    def edge_cells(c, at=0):
        return pl.ds(at + c, SUB, stride=SUB)

    for s in range(2):
        kcol_s[s] = kb[edge_cells(edge_col[s], PAD), :]

        @pl.when(has[s])
        def _():
            kcol_copy(s).start()
    krow_copy().start()

    sub_id = lax.broadcasted_iota(jnp.int32, (SUB, LANES), 0)
    no_w = jnp.where(has[0], 0.0, 1.0)
    no_e = jnp.where(has[1], 0.0, 1.0)

    def coeff_row(q, carry):
        base = pl.multiple_of(q * SUB, SUB)
        here = kb[pl.ds(PAD + base, SUB)]
        up = kb[pl.ds(base, SUB)]
        down = kb[pl.ds(2 * PAD + base, SUB)]
        left = jnp.concatenate([here[:1], here[:-1]], axis=0)
        right = jnp.concatenate([here[1:], here[-1:]], axis=0)
        vn = jnp.where(q == 0, 0.0, 1.0) * (0.5 * (here + up))
        vs = jnp.where(q == SUB - 1, 0.0, 1.0) * (0.5 * (here + down))
        vw = jnp.where(sub_id == 0, 0.0, 0.5 * (here + left))
        ve = jnp.where(sub_id == SUB - 1, 0.0, 0.5 * (here + right))
        rim = jnp.where(jnp.logical_or(jnp.logical_and(q == 0, row == 0),
                                       jnp.logical_and(q == SUB - 1, row == 1)), 1.0, 0.0)
        rim_col = jnp.where(sub_id == 0, no_w, 0.0) + jnp.where(sub_id == SUB - 1, no_e, 0.0)
        rows = pl.ds(base, SUB)
        cn[rows] = vn
        cs[rows] = vs
        cw[rows] = vw
        ce[rows] = ve
        cd[rows] = vn + vs + vw + ve + (rim + rim_col) * here
        return carry

    lax.fori_loop(0, SUB, coeff_row, 0)

    def stencil(g):
        def one_row(q, carry):
            base = pl.multiple_of(q * SUB, SUB)
            rows = pl.ds(base, SUB)
            vd, vn, vs, vw, ve = cd[rows], cn[rows], cs[rows], cw[rows], ce[rows]
            for t in range(TILES):
                k = g * TILES + t
                part = (vd * zf[k, pl.ds(PAD + base, SUB)]
                        - vn * zf[k, pl.ds(base, SUB)]
                        - vs * zf[k, pl.ds(2 * PAD + base, SUB)]
                        - vw * zf[k, pl.ds(PAD - 1 + base, SUB)]
                        - ve * zf[k, pl.ds(PAD + 1 + base, SUB)])
                res[k, rows] = res[k, rows] - part
            return carry

        lax.fori_loop(0, SUB, one_row, 0)

    def zrow_copy(g):
        return pltpu.make_async_remote_copy(
            zf.at[pl.ds(g * TILES, TILES), pl.ds(PAD + brow * SUB, SUB)], zrow.at[pl.ds(g * TILES, TILES)],
            sz_sem.at[g], rz_sem.at[g], device_id=partner, device_id_type=MESH)

    def row_fix(g):
        rows = pl.ds(pl.multiple_of(brow * SUB, SUB), SUB)
        zrows = pl.ds(pl.multiple_of(PAD + brow * SUB, SUB), SUB)
        for t in range(TILES):
            k = g * TILES + t
            res[k, rows] = res[k, rows] - crow[...] * (zf[k, zrows] - zrow[k])

    def p_copy(g, s, slot):
        return pltpu.make_async_remote_copy(send_p.at[g, s], recv_p.at[slot, g, 1 - s], sp_sem.at[g, s],
                                            rp_sem.at[slot, g, 1 - s], device_id=side_dev[s], device_id_type=MESH)

    def b_copy(g, s, slot, first=0):
        rows = pl.ds(first, 128 - first)
        return pltpu.make_async_remote_copy(send_b.at[g, s, rows], recv_b.at[slot, g, 1 - s, rows], sb_sem.at[g, s],
                                            rb_sem.at[slot, g, 1 - s], device_id=side_dev[s], device_id_type=MESH)

    def u_copy(g, s):
        return pltpu.make_async_remote_copy(send_u.at[g, s], recv_u.at[g, 1 - s], su_sem.at[g, s],
                                            ru_sem.at[g, 1 - s], device_id=side_dev[s], device_id_type=MESH)

    def near(s, dist):
        return dist if s == 0 else SUB - 1 - dist

    def fill_edges(g, first):
        for s in range(2):
            for t in range(TILES):
                k = g * TILES + t
                lanes = pl.ds(t * LANES, LANES)
                send_p[g, s, :, lanes] = res[k, edge_cells(near(s, 0)), :]
                zedge = zf[k, edge_cells(near(s, 0), PAD), :]
                if first:
                    send_u[g, s, :, lanes] = zedge
                else:
                    send_b[g, s, pl.ds(0, SUB), lanes] = zedge.astype(BF16)
                for d in range(1, MARGIN):
                    send_b[g, s, pl.ds(d * SUB, SUB), lanes] = res[k, edge_cells(near(s, d)), :].astype(BF16)

    def fwd_copies(g):
        rows = pl.multiple_of((SUB - MARGIN) * SUB * (1 - row), 128)
        half = pl.multiple_of(COLS_AT + 128 * (1 - row), 128)
        return [
            pltpu.make_async_remote_copy(e_v.at[g, pl.ds(rows, 128)], e_v.at[g, pl.ds(ROWS_AT, 128)],
                                         sf_sem.at[g, 0], rf_sem.at[g, 0], device_id=partner, device_id_type=MESH),
            pltpu.make_async_remote_copy(e_v.at[g, pl.ds(half, 128)], e_v.at[g, pl.ds(CORN_AT, 128)],
                                         sf_sem.at[g, 1], rf_sem.at[g, 1], device_id=partner, device_id_type=MESH)]

    def assemble(g, slot, first):
        for s in range(2):
            @pl.when(has[s])
            def _():
                p_copy(g, 1 - s, slot).wait_recv()
                if first:
                    u_copy(g, 1 - s).wait_recv()
                    b_copy(g, 1 - s, slot, SUB).wait_recv()
                else:
                    b_copy(g, 1 - s, slot).wait_recv()
                for t in range(TILES):
                    k = g * TILES + t
                    lanes = pl.ds(t * LANES, LANES)
                    if first:
                        theirs = recv_u[g, s, :, lanes]
                    else:
                        theirs = recv_b[slot, g, s, pl.ds(0, SUB), lanes].astype(F32)
                    cells = edge_cells(edge_col[s])
                    flux = cedge[s] * (zf[k, edge_cells(edge_col[s], PAD), :] - theirs)
                    res[k, cells, :] = res[k, cells, :] - flux
                    halo = (recv_p[slot, g, s, :, lanes] + flux).astype(BF16)
                    for h in range(2):
                        at = COLS_AT + 128 * h + 64 * s
                        e_v[g, pl.ds(at, 16), lanes] = halo[16 * h:16 * h + 16]
                        for d in range(1, MARGIN):
                            e_v[g, pl.ds(at + 16 * d, 16), lanes] = recv_b[slot, g, s, pl.ds(SUB * d + 16 * h, 16), lanes]

        def pack(q, carry):
            rows = pl.ds(pl.multiple_of(q * 64, 64), 64)
            for t in range(TILES):
                e_v[g, rows, pl.ds(t * LANES, LANES)] = res[g * TILES + t, rows].astype(BF16)
            return carry

        lax.fori_loop(0, CELLS // 64, pack, 0)
        for c in fwd_copies(g):
            c.start()

    def solve(g, last):
        for c in fwd_copies(g):
            c.wait()

        def rows_of(m, carry):
            rows = pl.ds(pl.multiple_of(m * 256, 256), 256)
            zrows = pl.ds(pl.multiple_of(PAD + m * 256, PAD), 256)
            z = jnp.dot(mat_p[rows, :], e_v[g], preferred_element_type=F32).astype(BF16).astype(F32)
            for t in range(TILES):
                k = g * TILES + t
                zt = z[:, t * LANES:(t + 1) * LANES]
                if last:
                    out_ref[rows, pl.ds(k * LANES, LANES)] = u_v[k, rows] + om * zt
                else:
                    zf[k, zrows] = zt
                    u_v[k, rows] = u_v[k, rows] + om * zt
            return carry

        lax.fori_loop(0, CELLS // 256, rows_of, 0)

    for k in range(groups * TILES):
        zf[k, pl.ds(0, PAD)] = zero_row
        zf[k, pl.ds(PAD + CELLS, PAD)] = zero_row
    for g in range(groups):
        e_v[g, pl.ds(COLS_AT, 256)] = jnp.zeros((256, GROUP), BF16)

    krow_copy().wait()
    rows_b = pl.ds(pl.multiple_of(PAD + brow * SUB, SUB), SUB)
    crow[...] = 0.5 * (kb[rows_b] + krow_r[...])

    for g in range(groups):
        for t in range(TILES):
            loads[g * TILES + t][0].wait()
        zrow_copy(g).start()
        for t in range(TILES):
            loads[g * TILES + t][1].wait()
        stencil(g)
        zrow_copy(g).wait()
        row_fix(g)
        fill_edges(g, True)
        for s in range(2):
            @pl.when(has[s])
            def _():
                p_copy(g, s, 0).start()
                u_copy(g, s).start()
                b_copy(g, s, 0, SUB).start()

    mat_copy.wait()

    def place(at, width, start, window, source, ok=None):
        n = lax.broadcasted_iota(jnp.int32, (window, width), 1)
        k = lax.broadcasted_iota(jnp.int32, (window, width), 0) + start
        pick = source(n) == k
        if ok is not None:
            pick = jnp.logical_and(pick, ok(n))
        pick = jnp.where(pick, 1.0, 0.0).astype(BF16)

        def rows_of(m, carry):
            rows = pl.ds(pl.multiple_of(m * 256, 256), 256)
            mat_p[rows, pl.ds(at, width)] = jnp.dot(mat_v[rows, pl.ds(start, window)], pick,
                                                    preferred_element_type=F32).astype(BF16)
            return carry

        lax.fori_loop(0, CELLS // 256, rows_of, 0)

    for q in range(4):
        low = (320 * q + 164) // 128 * 128
        high = -(-(320 * q + 476) // 128) * 128
        place(256 * q, 256, low, high - low, lambda n, q=q: own_source(n + 256 * q))

    def side_source(n):
        r = 16 * (n >> 7) + (n & 15)
        return (r + MARGIN) * EXT + side_column((n >> 6) & 1, (n >> 4) & 3)

    place(COLS_AT, 256, 128, 1408, side_source)

    def row_source(n):
        m = n & 127
        first_row = jnp.where(row == 0, MARGIN + SUB, 0)
        halo = (first_row + (m >> 5)) * EXT + MARGIN + (m & 31)
        corner_row = jnp.where(row == 0, MARGIN + SUB, -12) + (m & 15)
        corner = corner_row * EXT + side_column((m >> 6) & 1, (m >> 4) & 3)
        return jnp.where(n < 128, halo, corner)

    def row_ok(n):
        r16 = n & 15
        return jnp.logical_or(n < 128, jnp.where(row == 0, r16, 15 - r16) < MARGIN)

    place(ROWS_AT, 256, pl.multiple_of(1408 * (1 - row), 128), 192, row_source, row_ok)

    for s in range(2):
        @pl.when(has[s])
        def _():
            kcol_copy(1 - s).wait_recv()
            cedge[s] = 0.5 * (kcol_s[s] + kcol_r[s])
            kcol_copy(s).wait_send()
    for k in range(groups * TILES):
        loads[k][2].wait()

    for g in range(groups):
        assemble(g, 0, True)
    for s in range(2):
        @pl.when(has[s])
        def _():
            cedge[s] = om * cedge[s]
    crow[...] = om * crow[...]

    def scale(q, carry):
        rows = pl.ds(pl.multiple_of(q * SUB, SUB), SUB)
        for c in (cd, cn, cs, cw, ce):
            c[rows] = om * c[rows]
        return carry

    lax.fori_loop(0, SUB, scale, 0)

    def wait_sends(g, first):
        for s in range(2):
            @pl.when(has[s])
            def _():
                p_copy(g, s, 0).wait_send()
                if first:
                    u_copy(g, s).wait_send()
                    b_copy(g, s, 0, SUB).wait_send()
                else:
                    b_copy(g, s, 0).wait_send()

    def advance(g, slot, first):
        solve(g, False)
        zrow_copy(g).start()
        stencil(g)
        wait_sends(g, first)
        zrow_copy(g).wait()
        row_fix(g)
        fill_edges(g, False)
        for s in range(2):
            @pl.when(has[s])
            def _():
                p_copy(g, s, slot).start()
                b_copy(g, s, slot).start()

    for g in range(groups):
        advance(g, 1, True)

    def sweep(t, carry):
        slot = lax.rem(t, 2)
        for g in range(groups):
            assemble(g, 1 - slot, False)
            advance(g, slot, False)
        return carry

    lax.fori_loop(2, SWEEPS, sweep, 0)
    for g in range(groups):
        assemble(g, (SWEEPS - 1) % 2, False)
        solve(g, True)
    for g in range(groups):
        wait_sends(g, False)


def solution(mesh):
    col_count = mesh.shape['col']
    grid_spec = P('row', 'col', None)

    def device_fn(f_blk, u_blk, kappa_blk, mat_blk, omega_relax):
        rhs_count = u_blk.shape[2]
        groups = rhs_count // GROUP
        tiles = rhs_count // LANES
        vm = pltpu.VMEM
        dma = pltpu.SemaphoreType.DMA
        coeff = vm((CELLS, LANES), F32)
        out = pl.pallas_call(
            functools.partial(kernel, groups, col_count),
            out_shape=jax.ShapeDtypeStruct((CELLS, rhs_count), F32),
            in_specs=[pl.BlockSpec(memory_space=pl.ANY), pl.BlockSpec(memory_space=pl.ANY),
                      pl.BlockSpec(memory_space=pltpu.VMEM), pl.BlockSpec(memory_space=pl.ANY),
                      pl.BlockSpec(memory_space=pltpu.SMEM)],
            out_specs=pl.BlockSpec(memory_space=pltpu.VMEM),
            scratch_shapes=[
                vm((CELLS, EXT * EXT), BF16),
                vm((CELLS, DEPTH), BF16),
                vm((tiles, CELLS, LANES), F32),
                vm((tiles, CELLS + 2 * PAD, LANES), F32),
                vm((tiles, CELLS, LANES), F32),
                vm((groups, DEPTH, GROUP), BF16),
                vm((CELLS + 2 * PAD, LANES), F32),
                coeff, coeff, coeff, coeff, coeff,
                vm((2, SUB, LANES), F32),
                vm((SUB, LANES), F32),
                vm((groups, 2, SUB, GROUP), F32),
                vm((groups, 2, 128, GROUP), BF16),
                vm((groups, 2, SUB, GROUP), F32),
                vm((2, groups, 2, SUB, GROUP), F32),
                vm((2, groups, 2, 128, GROUP), BF16),
                vm((groups, 2, SUB, GROUP), F32),
                vm((tiles, SUB, LANES), F32),
                vm((2, SUB, LANES), F32),
                vm((2, SUB, LANES), F32),
                vm((SUB, LANES), F32),
                dma((3, tiles)), dma,
                dma((groups, 2)), dma((2, groups, 2)),
                dma((groups, 2)), dma((2, groups, 2)),
                dma((groups, 2)), dma((groups, 2)),
                dma((groups,)), dma((groups,)),
                dma((groups, 2)), dma((groups, 2)),
                dma((3,)), dma((3,)),
            ],
            compiler_params=pltpu.CompilerParams(collective_id=0, has_side_effects=True,
                                                 vmem_limit_bytes=60 * 1024 * 1024),
        )(f_blk.reshape(CELLS, rhs_count), u_blk.reshape(CELLS, rhs_count), kappa_blk,
          mat_blk.reshape(CELLS, EXT * EXT), omega_relax.reshape(1))
        return out.reshape(SUB, SUB, rhs_count)

    return jax.shard_map(device_fn, mesh=mesh,
                         in_specs=(grid_spec, grid_spec, P('row', 'col'), P('row', 'col', None, None), P()),
                         out_specs=grid_spec, check_vma=False)
```

time: 256 us -> 85.8 us (0.34)
  starting transfers between devices: 106 us -> 0 us
  waiting for transfers between devices: 77.2 us -> 0 us
  Pallas kernels: 0 us -> 74.9 us
  other arithmetic: 32.8 us -> 0 us
  matrix products: 14 us -> 0 us
  local copies, waits for them, and re-layouts: 21.9 us -> 8.63 us
    ppermute x52 -> x0, starting transfers between devices: 106 us -> none  [shift_from(): return lax.ppermute(values, axis_name, pair_list)]
    ppermute x52 -> x0, waiting for transfers between devices: 77.2 us -> none  [shift_from(): return lax.ppermute(values, axis_name, pair_list)]
    pallas_call x0 -> x1, Pallas kernels: none -> 74.9 us  [device_fn(): pl.pallas_call(functools.partial(kernel, groups, col_count), out_shape=ja...]
    slice x32 -> x0, local copies, waits for them, and re-layouts: 19 us -> none  [the longest x5 7.29 us: apply_local(): up_nb = jnp.concatenate([from_above, center[:-1]], axis=0)]
    convert_element_type x26 -> x0, other arithmetic: 16 us -> none  [the longest x6 15.2 us: device_fn(): residual.astype(jnp.bfloat16)]
    dot_general x6 -> x0, matrix products: 14 us -> none  [device_fn(): jnp.dot(solve_mat, ext_block.reshape(ext_cells, rhs_count), preferred_ele...]
    unnamed x22 -> x2, local copies, waits for them, and re-layouts: 0.04 us -> 8.63 us
    concatenate x6 -> x0, other arithmetic: 7.12 us -> none  [extend_block(): return jnp.concatenate([left_strip, tall_ext, right_strip], axis=1)]
  transfers between devices with their start and end apart: 52 -> 0, of which waited for: 28 -> 0; matrix products, arithmetic and copies ran while one was open for 7% -> 0% of each run, Pallas kernels for 0% -> 0%
where the time goes in v1:
time: 85.8 us; the launch traced here: 84.2 us
  Pallas kernels  74.9 us (87%)
  local copies, waits for them, and re-layouts  8.63 us (10%)
    pallas_call x1, Pallas kernels, device_fn(): pl.pallas_call(functools.partial(kernel, groups, col_count), out_shape=ja...  74.9 us
    unnamed x2, local copies, waits for them, and re-layouts  8.63 us

profile of v1, /device:TPU:0, one launch (start us, length us, event | category | flops | bytes accessed | tf_op | source)
XLA Modules:
  0.0 84.2 jit_solution(14666435449653679394)
XLA Ops:
  0.7 5.4 %copy.6 = bf16[1,1,1024,1600]{3,2,1,0:T(8,128)(2,1)} copy(bf16[1,1,1024,1600]{2,3,1,0:T(8,128)(2,1)} %param.8) | data formatting | bytes 6553600 | tf_op args[3]
  6.1 74.9 %shard_map.55 = f32[1024,512]{1,0:T(8,128)} custom-call(f32[1024,512]{1,0:T(8,128)} %bitcast.8, f32[1024,512]{1,0:T(8,128)} %bitcast.9, f32[32,32]{1,0:T(8,128)} %kap_ref.1, bf16[1024,1600]{1,0:T(8,128)(2,1)} %bitcast.6, f32[1]{0:T(128)} %bitcast.5.om_ref), custom_call_target="tpu_custom_call" | custom-call | tf_op jit(solution)/shard_map/pallas_call | solution.py:405
  81.0 3.2 %copy.9 = f32[32,32,512]{2,1,0:T(8,128)} copy(f32[32,32,512]{2,1,0:T(8,128)} %bitcast.7) | data formatting | bytes 4194304

commit v2 on v1

--- a/solution.py
+++ b/solution.py
@@ -33,10 +33,10 @@
 
 
 def kernel(groups, col_count,
-           f_hbm, u_hbm, kap_ref, mat_hbm, om_ref, out_ref,
-           mat_v, mat_p, res, zf, u_v, e_v, kb, cd, cn, cs, cw, ce, cedge, crow,
-           send_p, send_b, send_u, recv_p, recv_b, recv_u, zrow, kcol_s, kcol_r, krow_r,
-           in_sem, mat_sem, sp_sem, rp_sem, sb_sem, rb_sem, su_sem, ru_sem,
+           f_hbm, u_hbm, kap_ref, mat_hbm, om_ref, u_out, z_out,
+           mat_v, mat_p, acc, res, zf, u_v, e_v, z_v, kb, cd, cn, cs, cw, ce, cedge, cedge_om, crow,
+           send_p, send_b, send_u, recv_p, recv_b, recv_u, zrow_s, zrow, kcol_s, kcol_r, krow_r,
+           in_sem, mat_sem, out_sem, s_sem, r_sem, su_sem, ru_sem,
            sz_sem, rz_sem, sf_sem, rf_sem, sk_sem, rk_sem):
     col = lax.axis_index('col')
     row = lax.axis_index('row')
@@ -128,64 +128,93 @@
 
     lax.fori_loop(0, SUB, coeff_row, 0)
 
-    def stencil(g):
+    def stencil(g, first, count, unroll):
         def one_row(q, carry):
-            base = pl.multiple_of(q * SUB, SUB)
-            rows = pl.ds(base, SUB)
-            vd, vn, vs, vw, ve = cd[rows], cn[rows], cs[rows], cw[rows], ce[rows]
-            for t in range(TILES):
-                k = g * TILES + t
-                part = (vd * zf[k, pl.ds(PAD + base, SUB)]
-                        - vn * zf[k, pl.ds(base, SUB)]
-                        - vs * zf[k, pl.ds(2 * PAD + base, SUB)]
-                        - vw * zf[k, pl.ds(PAD - 1 + base, SUB)]
-                        - ve * zf[k, pl.ds(PAD + 1 + base, SUB)])
-                res[k, rows] = res[k, rows] - part
+            for at, n in zip(first, count):
+                base = pl.multiple_of(q * SUB + at, 8)
+                rows = pl.ds(base, n)
+                vd, vn, vs, vw, ve = cd[rows], cn[rows], cs[rows], cw[rows], ce[rows]
+                for t in range(TILES):
+                    k = g * TILES + t
+                    part = (vd * zf[k, pl.ds(PAD + base, n)]
+                            - vn * zf[k, pl.ds(base, n)]
+                            - vs * zf[k, pl.ds(2 * PAD + base, n)]
+                            - vw * zf[k, pl.ds(PAD - 1 + base, n)]
+                            - ve * zf[k, pl.ds(PAD + 1 + base, n)])
+                    res[k, rows] = res[k, rows] - part
             return carry
 
-        lax.fori_loop(0, SUB, one_row, 0)
+        lax.fori_loop(0, SUB, one_row, 0, unroll=unroll)
+
+    def stencil_sides(g):
+        stencil(g, (0, SUB - 8), (8, 8), 4)
+
+    def stencil_middle(g):
+        stencil(g, (8,), (16,), 4)
 
     def zrow_copy(g):
         return pltpu.make_async_remote_copy(
-            zf.at[pl.ds(g * TILES, TILES), pl.ds(PAD + brow * SUB, SUB)], zrow.at[pl.ds(g * TILES, TILES)],
-            sz_sem.at[g], rz_sem.at[g], device_id=partner, device_id_type=MESH)
+            zrow_s.at[g], zrow.at[g], sz_sem.at[g], rz_sem.at[g], device_id=partner, device_id_type=MESH)
+
+    brows = pl.ds(pl.multiple_of(brow * SUB, SUB), SUB)
 
     def row_fix(g):
-        rows = pl.ds(pl.multiple_of(brow * SUB, SUB), SUB)
-        zrows = pl.ds(pl.multiple_of(PAD + brow * SUB, SUB), SUB)
         for t in range(TILES):
             k = g * TILES + t
-            res[k, rows] = res[k, rows] - crow[...] * (zf[k, zrows] - zrow[k])
-
-    def p_copy(g, s, slot):
-        return pltpu.make_async_remote_copy(send_p.at[g, s], recv_p.at[slot, g, 1 - s], sp_sem.at[g, s],
-                                            rp_sem.at[slot, g, 1 - s], device_id=side_dev[s], device_id_type=MESH)
-
-    def b_copy(g, s, slot, first=0):
-        rows = pl.ds(first, 128 - first)
-        return pltpu.make_async_remote_copy(send_b.at[g, s, rows], recv_b.at[slot, g, 1 - s, rows], sb_sem.at[g, s],
-                                            rb_sem.at[slot, g, 1 - s], device_id=side_dev[s], device_id_type=MESH)
+            res[k, brows] = res[k, brows] - crow[...] * (zrow_s[g, t] - zrow[g, t])
+
+    def near(s, dist):
+        return dist if s == 0 else SUB - 1 - dist
+
+    far = row
+    closer = 1 - row
+
+    def message(g, s, slot, i):
+        half = (far, closer)[(i - 1) // 2]
+        if i in (1, 3):
+            rows = pl.ds(pl.multiple_of(16 * half, 16), 16)
+            src, dst = send_p, recv_p
+        else:
+            rows = pl.ds(0, SUB) if i == 0 else pl.ds(pl.multiple_of(SUB + 48 * half, 16), 48)
+            src, dst = send_b, recv_b
+        return pltpu.make_async_remote_copy(src.at[g, s, rows], dst.at[slot, g, 1 - s, rows], s_sem.at[g, s, i],
+                                            r_sem.at[slot, g, 1 - s, i], device_id=side_dev[s], device_id_type=MESH)
 
     def u_copy(g, s):
         return pltpu.make_async_remote_copy(send_u.at[g, s], recv_u.at[g, 1 - s], su_sem.at[g, s],
                                             ru_sem.at[g, 1 - s], device_id=side_dev[s], device_id_type=MESH)
 
-    def near(s, dist):
-        return dist if s == 0 else SUB - 1 - dist
-
-    def fill_edges(g, first):
+    def fill_z(g, first):
         for s in range(2):
             for t in range(TILES):
-                k = g * TILES + t
                 lanes = pl.ds(t * LANES, LANES)
-                send_p[g, s, :, lanes] = res[k, edge_cells(near(s, 0)), :]
-                zedge = zf[k, edge_cells(near(s, 0), PAD), :]
+                zedge = zf[g * TILES + t, edge_cells(near(s, 0), PAD), :]
                 if first:
                     send_u[g, s, :, lanes] = zedge
                 else:
                     send_b[g, s, pl.ds(0, SUB), lanes] = zedge.astype(BF16)
-                for d in range(1, MARGIN):
-                    send_b[g, s, pl.ds(d * SUB, SUB), lanes] = res[k, edge_cells(near(s, d)), :].astype(BF16)
+
+    def fill_half(g, h):
+        at = pl.multiple_of(CELLS // 2 * h, CELLS // 2)
+        p_at = pl.multiple_of(16 * h, 16)
+        e_at = pl.multiple_of(SUB + 48 * h, 16)
+        for s in range(2):
+            for t in range(TILES):
+                k = g * TILES + t
+                lanes = pl.ds(t * LANES, LANES)
+                for d in range(MARGIN):
+                    part = res[k, pl.ds(at + near(s, d), 16, stride=SUB), :]
+                    if d == 0:
+                        send_p[g, s, pl.ds(p_at, 16), lanes] = part
+                    else:
+                        send_b[g, s, pl.ds(e_at + 16 * (d - 1), 16), lanes] = part.astype(BF16)
+
+    def start(g, slot, which):
+        for s in range(2):
+            @pl.when(has[s])
+            def _():
+                for i in which:
+                    message(g, s, slot, i).start()
 
     def fwd_copies(g):
         rows = pl.multiple_of((SUB - MARGIN) * SUB * (1 - row), 128)
@@ -200,12 +229,10 @@
         for s in range(2):
             @pl.when(has[s])
             def _():
-                p_copy(g, 1 - s, slot).wait_recv()
                 if first:
                     u_copy(g, 1 - s).wait_recv()
-                    b_copy(g, 1 - s, slot, SUB).wait_recv()
-                else:
-                    b_copy(g, 1 - s, slot).wait_recv()
+                for i in range(1 if first else 0, 5):
+                    message(g, 1 - s, slot, i).wait_recv()
                 for t in range(TILES):
                     k = g * TILES + t
                     lanes = pl.ds(t * LANES, LANES)
@@ -214,44 +241,52 @@
                     else:
                         theirs = recv_b[slot, g, s, pl.ds(0, SUB), lanes].astype(F32)
                     cells = edge_cells(edge_col[s])
-                    flux = cedge[s] * (zf[k, edge_cells(edge_col[s], PAD), :] - theirs)
+                    coeff = cedge[s] if first else cedge_om[s]
+                    flux = coeff * (zf[k, edge_cells(edge_col[s], PAD), :] - theirs)
                     res[k, cells, :] = res[k, cells, :] - flux
                     halo = (recv_p[slot, g, s, :, lanes] + flux).astype(BF16)
                     for h in range(2):
                         at = COLS_AT + 128 * h + 64 * s
                         e_v[g, pl.ds(at, 16), lanes] = halo[16 * h:16 * h + 16]
-                        for d in range(1, MARGIN):
-                            e_v[g, pl.ds(at + 16 * d, 16), lanes] = recv_b[slot, g, s, pl.ds(SUB * d + 16 * h, 16), lanes]
-
-        def pack(q, carry):
+                        e_v[g, pl.ds(at + 16, 48), lanes] = recv_b[slot, g, s, pl.ds(SUB + 48 * h, 48), lanes]
+
+        def pack(rows):
+            for t in range(TILES):
+                e_v[g, rows, pl.ds(t * LANES, LANES)] = res[g * TILES + t, rows].astype(BF16)
+
+        fwd_rows, fwd_corners = fwd_copies(g)
+        fwd_corners.start()
+        pack(pl.ds(pl.multiple_of((SUB - MARGIN) * SUB * (1 - row), 128), 128))
+        rest = pl.multiple_of(128 * row, 128)
+
+        def pack_rest(q, carry):
+            pack(pl.ds(pl.multiple_of(rest + q * 128, 128), 128))
+            return carry
+
+        fwd_rows.start()
+        lax.fori_loop(0, CELLS // 128 - 1, pack_rest, 0)
+
+    def solve(g):
+        acc[...] = jnp.dot(mat_p[:, :ROWS_AT], e_v[g, pl.ds(0, ROWS_AT)], preferred_element_type=F32)
+        for c in fwd_copies(g):
+            c.wait()
+        acc[...] += jnp.dot(mat_p[:, ROWS_AT:], e_v[g, pl.ds(ROWS_AT, DEPTH - ROWS_AT)], preferred_element_type=F32)
+
+    def round_row(g):
+        for t in range(TILES):
+            zrow_s[g, t] = acc[brows, pl.ds(t * LANES, LANES)].astype(BF16).astype(F32)
+
+    def update(g):
+        def rows_of(q, carry):
             rows = pl.ds(pl.multiple_of(q * 64, 64), 64)
             for t in range(TILES):
-                e_v[g, rows, pl.ds(t * LANES, LANES)] = res[g * TILES + t, rows].astype(BF16)
+                k = g * TILES + t
+                z = acc[rows, pl.ds(t * LANES, LANES)].astype(BF16).astype(F32)
+                zf[k, pl.ds(pl.multiple_of(PAD + q * 64, PAD), 64)] = z
+                u_v[k, rows] = u_v[k, rows] + om * z
             return carry
 
-        lax.fori_loop(0, CELLS // 64, pack, 0)
-        for c in fwd_copies(g):
-            c.start()
-
-    def solve(g, last):
-        for c in fwd_copies(g):
-            c.wait()
-
-        def rows_of(m, carry):
-            rows = pl.ds(pl.multiple_of(m * 256, 256), 256)
-            zrows = pl.ds(pl.multiple_of(PAD + m * 256, PAD), 256)
-            z = jnp.dot(mat_p[rows, :], e_v[g], preferred_element_type=F32).astype(BF16).astype(F32)
-            for t in range(TILES):
-                k = g * TILES + t
-                zt = z[:, t * LANES:(t + 1) * LANES]
-                if last:
-                    out_ref[rows, pl.ds(k * LANES, LANES)] = u_v[k, rows] + om * zt
-                else:
-                    zf[k, zrows] = zt
-                    u_v[k, rows] = u_v[k, rows] + om * zt
-            return carry
-
-        lax.fori_loop(0, CELLS // 256, rows_of, 0)
+        lax.fori_loop(0, CELLS // 64, rows_of, 0)
 
     for k in range(groups * TILES):
         zf[k, pl.ds(0, PAD)] = zero_row
@@ -263,22 +298,30 @@
     rows_b = pl.ds(pl.multiple_of(PAD + brow * SUB, SUB), SUB)
     crow[...] = 0.5 * (kb[rows_b] + krow_r[...])
 
-    for g in range(groups):
-        for t in range(TILES):
-            loads[g * TILES + t][0].wait()
-        zrow_copy(g).start()
-        for t in range(TILES):
-            loads[g * TILES + t][1].wait()
-        stencil(g)
+    def send_bands(g, slot):
+        stencil_sides(g)
+        fill_half(g, far)
+        start(g, slot, (1, 2))
         zrow_copy(g).wait()
         row_fix(g)
-        fill_edges(g, True)
+        fill_half(g, closer)
+        start(g, slot, (3, 4))
+        stencil_middle(g)
+
+    for g in range(groups):
+        for t in range(TILES):
+            loads[g * TILES + t][0].wait()
+        for t in range(TILES):
+            zrow_s[g, t] = zf[g * TILES + t, rows_b]
+        zrow_copy(g).start()
+        fill_z(g, True)
         for s in range(2):
             @pl.when(has[s])
             def _():
-                p_copy(g, s, 0).start()
                 u_copy(g, s).start()
-                b_copy(g, s, 0, SUB).start()
+        for t in range(TILES):
+            loads[g * TILES + t][1].wait()
+        send_bands(g, 0)
 
     mat_copy.wait()
 
@@ -292,8 +335,9 @@
 
         def rows_of(m, carry):
             rows = pl.ds(pl.multiple_of(m * 256, 256), 256)
-            mat_p[rows, pl.ds(at, width)] = jnp.dot(mat_v[rows, pl.ds(start, window)], pick,
-                                                    preferred_element_type=F32).astype(BF16)
+            mat_p[rows, pl.ds(at, width)] = lax.dot_general(mat_v[pl.ds(start, window), rows], pick,
+                                                            (((0,), (0,)), ((), ())),
+                                                            preferred_element_type=F32).astype(BF16)
             return carry
 
         lax.fori_loop(0, CELLS // 256, rows_of, 0)
@@ -328,16 +372,8 @@
         def _():
             kcol_copy(1 - s).wait_recv()
             cedge[s] = 0.5 * (kcol_s[s] + kcol_r[s])
+            cedge_om[s] = om * cedge[s]
             kcol_copy(s).wait_send()
-    for k in range(groups * TILES):
-        loads[k][2].wait()
-
-    for g in range(groups):
-        assemble(g, 0, True)
-    for s in range(2):
-        @pl.when(has[s])
-        def _():
-            cedge[s] = om * cedge[s]
     crow[...] = om * crow[...]
 
     def scale(q, carry):
@@ -347,48 +383,63 @@
         return carry
 
     lax.fori_loop(0, SUB, scale, 0)
-
-    def wait_sends(g, first):
+    for k in range(groups * TILES):
+        loads[k][2].wait()
+
+    def wait_sends(g, which):
         for s in range(2):
             @pl.when(has[s])
             def _():
-                p_copy(g, s, 0).wait_send()
-                if first:
-                    u_copy(g, s).wait_send()
-                    b_copy(g, s, 0, SUB).wait_send()
-                else:
-                    b_copy(g, s, 0).wait_send()
+                for i in which:
+                    message(g, s, 0, i).wait_send()
 
     def advance(g, slot, first):
-        solve(g, False)
+        solve(g)
+        round_row(g)
         zrow_copy(g).start()
-        stencil(g)
-        wait_sends(g, first)
-        zrow_copy(g).wait()
-        row_fix(g)
-        fill_edges(g, False)
+        update(g)
+        if first:
+            wait_sends(g, (1, 2, 3, 4))
+        else:
+            wait_sends(g, (0, 1, 2, 3, 4))
+        fill_z(g, False)
+        start(g, slot, (0,))
+        send_bands(g, slot)
+
+    for g in range(groups):
+        assemble(g, 0, True)
+        advance(g, 1, True)
+
+    def step(i, carry):
+        t = i // groups
+        g = lax.rem(i, groups)
+        slot = lax.rem(t, 2)
+        assemble(g, 1 - slot, False)
+        advance(g, slot, False)
+        return carry
+
+    lax.fori_loop(2 * groups, SWEEPS * groups, step, 0)
+
+    u_copies = [pltpu.make_async_copy(u_v.at[k], u_out.at[:, pl.ds(k * LANES, LANES)], in_sem.at[0, k])
+                for k in range(groups * TILES)]
+    z_copies = [pltpu.make_async_copy(z_v.at[g], z_out.at[:, pl.ds(g * GROUP, GROUP)], out_sem.at[g])
+                for g in range(groups)]
+    for g in range(groups):
+        for t in range(TILES):
+            u_copies[g * TILES + t].start()
+    for g in range(groups):
+        assemble(g, (SWEEPS - 1) % 2, False)
+        solve(g)
+        z_v[g] = acc[...].astype(BF16)
+        z_copies[g].start()
+    for g in range(groups):
+        wait_sends(g, (0, 1, 2, 3, 4))
         for s in range(2):
             @pl.when(has[s])
             def _():
-                p_copy(g, s, slot).start()
-                b_copy(g, s, slot).start()
-
-    for g in range(groups):
-        advance(g, 1, True)
-
-    def sweep(t, carry):
-        slot = lax.rem(t, 2)
-        for g in range(groups):
-            assemble(g, 1 - slot, False)
-            advance(g, slot, False)
-        return carry
-
-    lax.fori_loop(2, SWEEPS, sweep, 0)
-    for g in range(groups):
-        assemble(g, (SWEEPS - 1) % 2, False)
-        solve(g, True)
-    for g in range(groups):
-        wait_sends(g, False)
+                u_copy(g, s).wait_send()
+    for c in u_copies + z_copies:
+        c.wait()
 
 
 def solution(mesh):
@@ -402,22 +453,25 @@
         vm = pltpu.VMEM
         dma = pltpu.SemaphoreType.DMA
         coeff = vm((CELLS, LANES), F32)
-        out = pl.pallas_call(
+        u_last, z_last = pl.pallas_call(
             functools.partial(kernel, groups, col_count),
-            out_shape=jax.ShapeDtypeStruct((CELLS, rhs_count), F32),
+            out_shape=(jax.ShapeDtypeStruct((CELLS, rhs_count), F32), jax.ShapeDtypeStruct((CELLS, rhs_count), BF16)),
             in_specs=[pl.BlockSpec(memory_space=pl.ANY), pl.BlockSpec(memory_space=pl.ANY),
                       pl.BlockSpec(memory_space=pltpu.VMEM), pl.BlockSpec(memory_space=pl.ANY),
                       pl.BlockSpec(memory_space=pltpu.SMEM)],
-            out_specs=pl.BlockSpec(memory_space=pltpu.VMEM),
+            out_specs=(pl.BlockSpec(memory_space=pl.ANY), pl.BlockSpec(memory_space=pl.ANY)),
             scratch_shapes=[
-                vm((CELLS, EXT * EXT), BF16),
+                vm((EXT * EXT, CELLS), BF16),
                 vm((CELLS, DEPTH), BF16),
+                vm((CELLS, GROUP), F32),
                 vm((tiles, CELLS, LANES), F32),
                 vm((tiles, CELLS + 2 * PAD, LANES), F32),
                 vm((tiles, CELLS, LANES), F32),
                 vm((groups, DEPTH, GROUP), BF16),
+                vm((groups, CELLS, GROUP), BF16),
                 vm((CELLS + 2 * PAD, LANES), F32),
                 coeff, coeff, coeff, coeff, coeff,
+                vm((2, SUB, LANES), F32),
                 vm((2, SUB, LANES), F32),
                 vm((SUB, LANES), F32),
                 vm((groups, 2, SUB, GROUP), F32),
@@ -426,13 +480,13 @@
                 vm((2, groups, 2, SUB, GROUP), F32),
                 vm((2, groups, 2, 128, GROUP), BF16),
                 vm((groups, 2, SUB, GROUP), F32),
-                vm((tiles, SUB, LANES), F32),
+                vm((groups, TILES, SUB, LANES), F32),
+                vm((groups, TILES, SUB, LANES), F32),
                 vm((2, SUB, LANES), F32),
                 vm((2, SUB, LANES), F32),
                 vm((SUB, LANES), F32),
-                dma((3, tiles)), dma,
-                dma((groups, 2)), dma((2, groups, 2)),
-                dma((groups, 2)), dma((2, groups, 2)),
+                dma((3, tiles)), dma, dma((groups,)),
+                dma((groups, 2, 5)), dma((2, groups, 2, 5)),
                 dma((groups, 2)), dma((groups, 2)),
                 dma((groups,)), dma((groups,)),
                 dma((groups, 2)), dma((groups, 2)),
@@ -441,8 +495,8 @@
             compiler_params=pltpu.CompilerParams(collective_id=0, has_side_effects=True,
                                                  vmem_limit_bytes=60 * 1024 * 1024),
         )(f_blk.reshape(CELLS, rhs_count), u_blk.reshape(CELLS, rhs_count), kappa_blk,
-          mat_blk.reshape(CELLS, EXT * EXT), omega_relax.reshape(1))
-        return out.reshape(SUB, SUB, rhs_count)
+          mat_blk.reshape(CELLS, EXT * EXT).T, omega_relax.reshape(1))
+        return (u_last + omega_relax * z_last.astype(F32)).reshape(SUB, SUB, rhs_count)
 
     return jax.shard_map(device_fn, mesh=mesh,
                          in_specs=(grid_spec, grid_spec, P('row', 'col'), P('row', 'col', None, None), P()),

time: 85.8 us -> 71.5 us (0.83); the launches traced: 84.2 us -> 71.4 us
  local copies, waits for them, and re-layouts: 8.63 us -> 0 us
  Pallas kernels: 74.9 us -> 67.2 us
  other arithmetic: 0 us -> 3.52 us
    unnamed x2 -> x0, local copies, waits for them, and re-layouts: 8.63 us -> none
    pallas_call x1, Pallas kernels: 74.9 us -> 67.2 us  [device_fn(): pl.pallas_call(functools.partial(kernel, groups, col_count), out_shape=(j...]
    add x0 -> x1, other arithmetic: none -> 3.52 us  [device_fn(): u_last + omega_relax * z_last.astype(F32)]
where the time goes in v2:
time: 71.5 us; the launch traced here: 71.4 us
  Pallas kernels  67.2 us (94%)
  other arithmetic  3.52 us (5%)
    pallas_call x1, Pallas kernels, device_fn(): pl.pallas_call(functools.partial(kernel, groups, col_count), out_shape=(j...  67.2 us
    add x1, other arithmetic, device_fn(): u_last + omega_relax * z_last.astype(F32)  3.52 us

profile of v2, /device:TPU:0, one launch (start us, length us, event | category | flops | bytes accessed | tf_op | source)
XLA Modules:
  0.0 71.4 jit_solution(5762791308105537744)
XLA Ops:
  0.7 67.2 %shard_map.55 = (f32[1024,512]{1,0:T(8,128)}, bf16[1024,512]{1,0:T(8,128)(2,1)}) custom-call(f32[1024,512]{1,0:T(8,128)} %bitcast.9, f32[1024,512]{1,0:T(8,128)} %bitcast.10, f32[32,32]{1,0:T(8,128)} %kap_ref.1, bf16[1600,1024]{1,0:T(8,128)(2,1)} %bitcast.8, f32[1]{0:T(128)} %bitcast.7.om_ref), custom_call_target="tpu_custom_call" | custom-call | tf_op jit(solution)/shard_map/pallas_call | solution.py:456
  67.8 3.5 %multiply_add_fusion = f32[1024,512]{1,0:T(8,128)} fusion(f32[1024,512]{1,0:T(8,128)} %get-tuple-element.7, bf16[1024,512]{1,0:T(8,128)(2,1)} %get-tuple-element.8, f32[]{:T(128)} %copy.6), kind=kLoop, calls=%fused_computation | loop fusion | flops 1572864 | bytes 5242884 | tf_op jit(solution)/shard_map/add | solution.py:499

commit v3 on v2

--- a/solution.py
+++ b/solution.py
@@ -34,7 +34,7 @@
 
 def kernel(groups, col_count,
            f_hbm, u_hbm, kap_ref, mat_hbm, om_ref, u_out, z_out,
-           mat_v, mat_p, acc, res, zf, u_v, e_v, z_v, kb, cd, cn, cs, cw, ce, cedge, cedge_om, crow,
+           mat_v, mat_t, mat_p, acc, res, zf, u_v, e_v, z_v, kb, cd, cn, cs, cw, ce, cedge, cedge_om, crow,
            send_p, send_b, send_u, recv_p, recv_b, recv_u, zrow_s, zrow, kcol_s, kcol_r, krow_r,
            in_sem, mat_sem, out_sem, s_sem, r_sem, su_sem, ru_sem,
            sz_sem, rz_sem, sf_sem, rf_sem, sk_sem, rk_sem):
@@ -324,6 +324,9 @@
         send_bands(g, 0)
 
     mat_copy.wait()
+    for at in range(0, EXT * EXT, 256):
+        span = pl.ds(at, min(256, EXT * EXT - at))
+        mat_t[:, span] = mat_v[span].T
 
     def place(at, width, start, window, source, ok=None):
         n = lax.broadcasted_iota(jnp.int32, (window, width), 1)
@@ -333,14 +336,8 @@
             pick = jnp.logical_and(pick, ok(n))
         pick = jnp.where(pick, 1.0, 0.0).astype(BF16)
 
-        def rows_of(m, carry):
-            rows = pl.ds(pl.multiple_of(m * 256, 256), 256)
-            mat_p[rows, pl.ds(at, width)] = lax.dot_general(mat_v[pl.ds(start, window), rows], pick,
-                                                            (((0,), (0,)), ((), ())),
-                                                            preferred_element_type=F32).astype(BF16)
-            return carry
-
-        lax.fori_loop(0, CELLS // 256, rows_of, 0)
+        acc[...] = jnp.dot(mat_t[:, pl.ds(start, window)], pick, preferred_element_type=F32)
+        mat_p[:, pl.ds(at, width)] = acc[...].astype(BF16)
 
     for q in range(4):
         low = (320 * q + 164) // 128 * 128
@@ -456,12 +453,13 @@
         u_last, z_last = pl.pallas_call(
             functools.partial(kernel, groups, col_count),
             out_shape=(jax.ShapeDtypeStruct((CELLS, rhs_count), F32), jax.ShapeDtypeStruct((CELLS, rhs_count), BF16)),
-            in_specs=[pl.BlockSpec(memory_space=pl.ANY), pl.BlockSpec(memory_space=pl.ANY),
-                      pl.BlockSpec(memory_space=pltpu.VMEM), pl.BlockSpec(memory_space=pl.ANY),
+            in_specs=[pl.BlockSpec(memory_space=pltpu.HBM), pl.BlockSpec(memory_space=pltpu.HBM),
+                      pl.BlockSpec(memory_space=pltpu.VMEM), pl.BlockSpec(memory_space=pltpu.HBM),
                       pl.BlockSpec(memory_space=pltpu.SMEM)],
             out_specs=(pl.BlockSpec(memory_space=pl.ANY), pl.BlockSpec(memory_space=pl.ANY)),
             scratch_shapes=[
                 vm((EXT * EXT, CELLS), BF16),
+                vm((CELLS, EXT * EXT), BF16),
                 vm((CELLS, DEPTH), BF16),
                 vm((CELLS, GROUP), F32),
                 vm((tiles, CELLS, LANES), F32),
@@ -493,7 +491,7 @@
                 dma((3,)), dma((3,)),
             ],
             compiler_params=pltpu.CompilerParams(collective_id=0, has_side_effects=True,
-                                                 vmem_limit_bytes=60 * 1024 * 1024),
+                                                 vmem_limit_bytes=50 * 1024 * 1024),
         )(f_blk.reshape(CELLS, rhs_count), u_blk.reshape(CELLS, rhs_count), kappa_blk,
           mat_blk.reshape(CELLS, EXT * EXT).T, omega_relax.reshape(1))
         return (u_last + omega_relax * z_last.astype(F32)).reshape(SUB, SUB, rhs_count)

time: 71.5 us -> 65.9 us (0.922)
  Pallas kernels: 67.2 us -> 62.7 us
  other arithmetic: 3.52 us -> 1.66 us
    pallas_call x1, Pallas kernels: 67.2 us -> 62.7 us  [device_fn(): pl.pallas_call(functools.partial(kernel, groups, col_count), out_shape=(j...]
    add x1, other arithmetic: 3.52 us -> 1.66 us  [device_fn(): u_last + omega_relax * z_last.astype(F32)]
where the time goes in v3:
time: 65.9 us; the launch traced here: 65.7 us
  Pallas kernels  62.7 us (95%)
  other arithmetic  1.66 us (3%)
  local copies, waits for them, and re-layouts  0.71 us (1%)
  between operations  0.67 us (1%)
    pallas_call x1, Pallas kernels, device_fn(): pl.pallas_call(functools.partial(kernel, groups, col_count), out_shape=(j...  62.7 us
    add x1, other arithmetic, device_fn(): u_last + omega_relax * z_last.astype(F32)  1.66 us

profile of v3, /device:TPU:0, one launch (start us, length us, event | category | flops | bytes accessed | tf_op | source)
XLA Modules:
  0.0 65.7 jit_solution(17447558155614907351)
XLA Ops:
  0.7 0.0 copy-start
  0.7 0.7 %copy-done = f32[32,32]{1,0:T(8,128)S(1)} copy-done((f32[32,32]{1,0:T(8,128)S(1)}, f32[32,32]{1,0:T(8,128)}, u32[]{:S(2)}) %copy-start) | copy-done | bytes 4120
  1.4 62.7 %shard_map.55 = (f32[1024,512]{1,0:T(8,128)S(1)}, bf16[1024,512]{1,0:T(8,128)(2,1)S(1)}) custom-call(f32[1024,512]{1,0:T(8,128)} %bitcast.9, f32[1024,512]{1,0:T(8,128)} %bitcast.10, f32[32,32]{1,0:T(8,128)S(1)} %copy-done, bf16[1600,1024]{1,0:T(8,128)(2,1)} %bitcast.8, f32[1]{0:T(128)} %bitcast.7.om_ref), custom_call_target="tpu_custom_call" | custom-call | tf_op jit(solution)/shard_map/pallas_call | solution.py:453
  64.1 1.7 %multiply_add_fusion = f32[1024,512]{1,0:T(8,128)} fusion(f32[1024,512]{1,0:T(8,128)S(1)} %get-tuple-element.7, bf16[1024,512]{1,0:T(8,128)(2,1)S(1)} %get-tuple-element.8, f32[]{:T(128)} %copy.6), kind=kLoop, calls=%fused_computation | loop fusion | flops 1572864 | bytes 5242884 | tf_op jit(solution)/shard_map/add | solution.py:497
Async XLA Ops:
  0.7 0.7 %copy-start = (f32[32,32]{1,0:T(8,128)S(1)}, f32[32,32]{1,0:T(8,128)}, u32[]{:S(2)}) copy-start(f32[32,32]{1,0:T(8,128)} %kap_ref.1) | copy-start | bytes 12292

commit v4 on v3

--- a/solution.py
+++ b/solution.py
@@ -28,6 +28,10 @@
     return ((n >> 5) + MARGIN) * EXT + (n & 31) + MARGIN
 
 
+def mod(t, n):
+    return t % n if isinstance(t, int) else lax.rem(t, n)
+
+
 def side_column(side, dist):
     return jnp.where(side == 0, MARGIN - 1 - dist, MARGIN + SUB + dist)
 
@@ -36,8 +40,9 @@
            f_hbm, u_hbm, kap_ref, mat_hbm, om_ref, u_out, z_out,
            mat_v, mat_t, mat_p, acc, res, zf, u_v, e_v, z_v, kb, cd, cn, cs, cw, ce, cedge, cedge_om, crow,
            send_p, send_b, send_u, recv_p, recv_b, recv_u, zrow_s, zrow, kcol_s, kcol_r, krow_r,
-           in_sem, mat_sem, out_sem, s_sem, r_sem, su_sem, ru_sem,
-           sz_sem, rz_sem, sf_sem, rf_sem, sk_sem, rk_sem):
+           via_p, via_b, via_u,
+           in_sem, mat_sem, out_sem, s_sem, r_sem,
+           sz_sem, rz_sem, sf_sem, rf_sem, sk_sem, rk_sem, vs_sem, vr_sem):
     col = lax.axis_index('col')
     row = lax.axis_index('row')
     has = (col > 0, col < col_count - 1)
@@ -45,6 +50,13 @@
     partner = (col, 1 - row)
     brow = (SUB - 1) * (1 - row)
     om = om_ref[0]
+
+    routed = row == 1
+    detour = (jnp.logical_and(routed, col == 2), jnp.logical_and(routed, col == 1))
+    is_via = jnp.logical_and(routed, jnp.logical_or(col == 0, col == 3))
+    mate = (lax.rem(col + 2, 4), row)
+    via_to = (jnp.where(col == 0, 1, 2), row)
+    via_side = jnp.where(col == 0, 1, 0)
 
     loads = []
     for g in range(groups):
@@ -69,7 +81,10 @@
         @pl.when(has[s])
         def _():
             pl.semaphore_signal(barrier, inc=1, device_id=side_dev[s], device_id_type=MESH)
-    waits = 1 + has[0].astype(jnp.int32) + has[1].astype(jnp.int32)
+    @pl.when(routed)
+    def _():
+        pl.semaphore_signal(barrier, inc=1, device_id=mate, device_id_type=MESH)
+    waits = 1 + has[0].astype(jnp.int32) + has[1].astype(jnp.int32) + routed.astype(jnp.int32)
     pl.semaphore_wait(barrier, waits)
 
     zero_row = jnp.zeros((SUB, LANES), F32)
@@ -169,20 +184,47 @@
     far = row
     closer = 1 - row
 
-    def message(g, s, slot, i):
-        half = (far, closer)[(i - 1) // 2]
+    def part(g, i):
+        half = (far, closer)[(i - 1) // 2 % 2]
         if i in (1, 3):
-            rows = pl.ds(pl.multiple_of(16 * half, 16), 16)
-            src, dst = send_p, recv_p
-        else:
-            rows = pl.ds(0, SUB) if i == 0 else pl.ds(pl.multiple_of(SUB + 48 * half, 16), 48)
-            src, dst = send_b, recv_b
-        return pltpu.make_async_remote_copy(src.at[g, s, rows], dst.at[slot, g, 1 - s, rows], s_sem.at[g, s, i],
-                                            r_sem.at[slot, g, 1 - s, i], device_id=side_dev[s], device_id_type=MESH)
-
-    def u_copy(g, s):
-        return pltpu.make_async_remote_copy(send_u.at[g, s], recv_u.at[g, 1 - s], su_sem.at[g, s],
-                                            ru_sem.at[g, 1 - s], device_id=side_dev[s], device_id_type=MESH)
+            return 1, pl.ds(pl.multiple_of(16 * half, 16), 16)
+        if i in (2, 4):
+            return 0, pl.ds(pl.multiple_of(SUB + 48 * half, 16), 48)
+        return (0 if i == 0 else 2), pl.ds(0, SUB)
+
+    def message(g, s, t, i):
+        kind, rows = part(g, i)
+        slot = mod(t, 2)
+        src = (send_b, send_p, send_u)[kind].at[g, s, rows]
+        dst = (recv_b, recv_p, recv_u)[kind].at[slot, g, 1 - s, rows]
+        return pltpu.make_async_remote_copy(src, dst, s_sem.at[g, s, i], r_sem.at[slot, g, 1 - s, i],
+                                            device_id=side_dev[s], device_id_type=MESH)
+
+    def message_out(g, s, t, i):
+        kind, rows = part(g, i)
+        slot = mod(t, 3)
+        src = (send_b, send_p, send_u)[kind].at[g, s, rows]
+        dst = (via_b, via_p, via_u)[kind].at[slot, g, rows]
+        return pltpu.make_async_remote_copy(src, dst, s_sem.at[g, s, i], vr_sem.at[slot, g, i],
+                                            device_id=mate, device_id_type=MESH)
+
+    def message_on(g, t, i):
+        kind, rows = part(g, i)
+        slot = mod(t, 2)
+        src = (via_b, via_p, via_u)[kind].at[mod(t, 3), g, rows]
+        dst = (recv_b, recv_p, recv_u)[kind].at[slot, g, via_side, rows]
+        return pltpu.make_async_remote_copy(src, dst, vs_sem.at[g, i], r_sem.at[slot, g, via_side, i],
+                                            device_id=via_to, device_id_type=MESH)
+
+    SWEEP_PARTS = (0, 1, 2, 3, 4)
+    FIRST_PARTS = (5, 1, 2, 3, 4)
+
+    def pass_on(g, t, parts):
+        @pl.when(is_via)
+        def _():
+            for i in parts:
+                message_out(g, 0, t, i).wait_recv()
+                message_on(g, t, i).start()
 
     def fill_z(g, first):
         for s in range(2):
@@ -209,12 +251,17 @@
                     else:
                         send_b[g, s, pl.ds(e_at + 16 * (d - 1), 16), lanes] = part.astype(BF16)
 
-    def start(g, slot, which):
+    def start(g, t, which):
         for s in range(2):
-            @pl.when(has[s])
+            @pl.when(jnp.logical_and(has[s], jnp.logical_not(detour[s])))
             def _():
                 for i in which:
-                    message(g, s, slot, i).start()
+                    message(g, s, t, i).start()
+
+            @pl.when(detour[s])
+            def _():
+                for i in which:
+                    message_out(g, s, t, i).start()
 
     def fwd_copies(g):
         rows = pl.multiple_of((SUB - MARGIN) * SUB * (1 - row), 128)
@@ -225,19 +272,18 @@
             pltpu.make_async_remote_copy(e_v.at[g, pl.ds(half, 128)], e_v.at[g, pl.ds(CORN_AT, 128)],
                                          sf_sem.at[g, 1], rf_sem.at[g, 1], device_id=partner, device_id_type=MESH)]
 
-    def assemble(g, slot, first):
+    def assemble(g, sent, first):
+        slot = mod(sent, 2)
         for s in range(2):
             @pl.when(has[s])
             def _():
-                if first:
-                    u_copy(g, 1 - s).wait_recv()
-                for i in range(1 if first else 0, 5):
-                    message(g, 1 - s, slot, i).wait_recv()
+                for i in FIRST_PARTS if first else SWEEP_PARTS:
+                    message(g, 1 - s, sent, i).wait_recv()
                 for t in range(TILES):
                     k = g * TILES + t
                     lanes = pl.ds(t * LANES, LANES)
                     if first:
-                        theirs = recv_u[g, s, :, lanes]
+                        theirs = recv_u[slot, g, s, :, lanes]
                     else:
                         theirs = recv_b[slot, g, s, pl.ds(0, SUB), lanes].astype(F32)
                     cells = edge_cells(edge_col[s])
@@ -298,14 +344,14 @@
     rows_b = pl.ds(pl.multiple_of(PAD + brow * SUB, SUB), SUB)
     crow[...] = 0.5 * (kb[rows_b] + krow_r[...])
 
-    def send_bands(g, slot):
+    def send_bands(g, t):
         stencil_sides(g)
         fill_half(g, far)
-        start(g, slot, (1, 2))
+        start(g, t, (1, 2))
         zrow_copy(g).wait()
         row_fix(g)
         fill_half(g, closer)
-        start(g, slot, (3, 4))
+        start(g, t, (3, 4))
         stencil_middle(g)
 
     for g in range(groups):
@@ -315,10 +361,7 @@
             zrow_s[g, t] = zf[g * TILES + t, rows_b]
         zrow_copy(g).start()
         fill_z(g, True)
-        for s in range(2):
-            @pl.when(has[s])
-            def _():
-                u_copy(g, s).start()
+        start(g, 0, (5,))
         for t in range(TILES):
             loads[g * TILES + t][1].wait()
         send_bands(g, 0)
@@ -327,6 +370,7 @@
     for at in range(0, EXT * EXT, 256):
         span = pl.ds(at, min(256, EXT * EXT - at))
         mat_t[:, span] = mat_v[span].T
+    pass_on(0, 0, FIRST_PARTS)
 
     def place(at, width, start, window, source, ok=None):
         n = lax.broadcasted_iota(jnp.int32, (window, width), 1)
@@ -348,6 +392,7 @@
         r = 16 * (n >> 7) + (n & 15)
         return (r + MARGIN) * EXT + side_column((n >> 6) & 1, (n >> 4) & 3)
 
+    pass_on(1, 0, FIRST_PARTS)
     place(COLS_AT, 256, 128, 1408, side_source)
 
     def row_source(n):
@@ -390,29 +435,33 @@
                 for i in which:
                     message(g, s, 0, i).wait_send()
 
-    def advance(g, slot, first):
+        @pl.when(is_via)
+        def _():
+            for i in which:
+                message_on(g, 0, i).wait_send()
+
+    def advance(g, t, first, relay):
         solve(g)
         round_row(g)
         zrow_copy(g).start()
         update(g)
-        if first:
-            wait_sends(g, (1, 2, 3, 4))
-        else:
-            wait_sends(g, (0, 1, 2, 3, 4))
+        wait_sends(g, FIRST_PARTS if first else SWEEP_PARTS)
         fill_z(g, False)
-        start(g, slot, (0,))
-        send_bands(g, slot)
-
-    for g in range(groups):
-        assemble(g, 0, True)
-        advance(g, 1, True)
+        start(g, t, (0,))
+        if relay is not None:
+            pass_on(*relay)
+        send_bands(g, t)
+
+    assemble(0, 0, True)
+    advance(0, 1, True, None)
+    assemble(1, 0, True)
+    advance(1, 1, True, (0, 1, SWEEP_PARTS))
 
     def step(i, carry):
         t = i // groups
         g = lax.rem(i, groups)
-        slot = lax.rem(t, 2)
-        assemble(g, 1 - slot, False)
-        advance(g, slot, False)
+        assemble(g, t - 1, False)
+        advance(g, t, False, (1 - g, jnp.where(g == 0, t - 1, t), SWEEP_PARTS))
         return carry
 
     lax.fori_loop(2 * groups, SWEEPS * groups, step, 0)
@@ -425,16 +474,14 @@
         for t in range(TILES):
             u_copies[g * TILES + t].start()
     for g in range(groups):
-        assemble(g, (SWEEPS - 1) % 2, False)
+        assemble(g, SWEEPS - 1, False)
         solve(g)
         z_v[g] = acc[...].astype(BF16)
         z_copies[g].start()
+        if g == 0:
+            pass_on(1, SWEEPS - 1, SWEEP_PARTS)
     for g in range(groups):
-        wait_sends(g, (0, 1, 2, 3, 4))
-        for s in range(2):
-            @pl.when(has[s])
-            def _():
-                u_copy(g, s).wait_send()
+        wait_sends(g, SWEEP_PARTS)
     for c in u_copies + z_copies:
         c.wait()
 
@@ -477,18 +524,21 @@
                 vm((groups, 2, SUB, GROUP), F32),
                 vm((2, groups, 2, SUB, GROUP), F32),
                 vm((2, groups, 2, 128, GROUP), BF16),
-                vm((groups, 2, SUB, GROUP), F32),
+                vm((1, groups, 2, SUB, GROUP), F32),
                 vm((groups, TILES, SUB, LANES), F32),
                 vm((groups, TILES, SUB, LANES), F32),
                 vm((2, SUB, LANES), F32),
                 vm((2, SUB, LANES), F32),
                 vm((SUB, LANES), F32),
+                vm((3, groups, SUB, GROUP), F32),
+                vm((3, groups, 128, GROUP), BF16),
+                vm((1, groups, SUB, GROUP), F32),
                 dma((3, tiles)), dma, dma((groups,)),
-                dma((groups, 2, 5)), dma((2, groups, 2, 5)),
-                dma((groups, 2)), dma((groups, 2)),
+                dma((groups, 2, 6)), dma((2, groups, 2, 6)),
                 dma((groups,)), dma((groups,)),
                 dma((groups, 2)), dma((groups, 2)),
                 dma((3,)), dma((3,)),
+                dma((groups, 6)), dma((3, groups, 6)),
             ],
             compiler_params=pltpu.CompilerParams(collective_id=0, has_side_effects=True,
                                                  vmem_limit_bytes=50 * 1024 * 1024),

time: 65.9 us -> 65.6 us (level)
  no operation moved by 1% of the time
where the time goes in v4:
time: 65.6 us; the launch traced here: 65.4 us
  Pallas kernels  62.3 us (95%)
  other arithmetic  1.66 us (3%)
  local copies, waits for them, and re-layouts  0.71 us (1%)
  between operations  0.67 us (1%)
    pallas_call x1, Pallas kernels, device_fn(): pl.pallas_call(functools.partial(kernel, groups, col_count), out_shape=(j...  62.3 us
    add x1, other arithmetic, device_fn(): u_last + omega_relax * z_last.astype(F32)  1.66 us

profile of v4, /device:TPU:0, one launch (start us, length us, event | category | flops | bytes accessed | tf_op | source)
XLA Modules:
  0.0 65.4 jit_solution(9203067765888133552)
XLA Ops:
  0.7 0.0 copy-start
  0.7 0.7 %copy-done = f32[32,32]{1,0:T(8,128)S(1)} copy-done((f32[32,32]{1,0:T(8,128)S(1)}, f32[32,32]{1,0:T(8,128)}, u32[]{:S(2)}) %copy-start) | copy-done | bytes 4120
  1.4 62.3 %shard_map.55 = (f32[1024,512]{1,0:T(8,128)S(1)}, bf16[1024,512]{1,0:T(8,128)(2,1)S(1)}) custom-call(f32[1024,512]{1,0:T(8,128)} %bitcast.9, f32[1024,512]{1,0:T(8,128)} %bitcast.10, f32[32,32]{1,0:T(8,128)S(1)} %copy-done, bf16[1600,1024]{1,0:T(8,128)(2,1)} %bitcast.8, f32[1]{0:T(128)} %bitcast.7.om_ref), custom_call_target="tpu_custom_call" | custom-call | tf_op jit(solution)/shard_map/pallas_call | solution.py:500
  63.7 1.7 %multiply_add_fusion = f32[1024,512]{1,0:T(8,128)} fusion(f32[1024,512]{1,0:T(8,128)S(1)} %get-tuple-element.7, bf16[1024,512]{1,0:T(8,128)(2,1)S(1)} %get-tuple-element.8, f32[]{:T(128)} %copy.6), kind=kLoop, calls=%fused_computation | loop fusion | flops 1572864 | bytes 5242884 | tf_op jit(solution)/shard_map/add | solution.py:547
Async XLA Ops:
  0.7 0.7 %copy-start = (f32[32,32]{1,0:T(8,128)S(1)}, f32[32,32]{1,0:T(8,128)}, u32[]{:S(2)}) copy-start(f32[32,32]{1,0:T(8,128)} %kap_ref.1) | copy-start | bytes 12292

commit v5 on v4

--- a/solution.py
+++ b/solution.py
@@ -14,10 +14,12 @@
 LANES = 128
 TILES = 2
 GROUP = TILES * LANES
+STEPS = MARGIN + 1
+HALF_COLS = 2 * STEPS * 16
 COLS_AT = CELLS
-ROWS_AT = CELLS + 256
+ROWS_AT = CELLS + 384
 CORN_AT = ROWS_AT + 128
-DEPTH = CORN_AT + 128
+DEPTH = CORN_AT + 256
 PAD = SUB
 MESH = pl.DeviceIdType.MESH
 F32 = jnp.float32
@@ -32,13 +34,15 @@
     return t % n if isinstance(t, int) else lax.rem(t, n)
 
 
-def side_column(side, dist):
-    return jnp.where(side == 0, MARGIN - 1 - dist, MARGIN + SUB + dist)
+def column_source(m):
+    side = m >= STEPS * 16
+    k = jnp.where(side, m - STEPS * 16, m)
+    return k & 15, jnp.where(side, MARGIN + SUB - 1 + (k >> 4), MARGIN - (k >> 4))
 
 
 def kernel(groups, col_count,
            f_hbm, u_hbm, kap_ref, mat_hbm, om_ref, u_out, z_out,
-           mat_v, mat_t, mat_p, acc, res, zf, u_v, e_v, z_v, kb, cd, cn, cs, cw, ce, cedge, cedge_om, crow,
+           mat_v, mat_t, mat_p, wide, acc, res, zf, u_v, e_v, z_v, kb, cd, cn, cs, cw, ce, cedge, cedge_om, crow,
            send_p, send_b, send_u, recv_p, recv_b, recv_u, zrow_s, zrow, kcol_s, kcol_r, krow_r,
            via_p, via_b, via_u,
            in_sem, mat_sem, out_sem, s_sem, r_sem,
@@ -185,7 +189,7 @@
     closer = 1 - row
 
     def part(g, i):
-        half = (far, closer)[(i - 1) // 2 % 2]
+        half = (closer, far)[(i - 1) // 2 % 2]
         if i in (1, 3):
             return 1, pl.ds(pl.multiple_of(16 * half, 16), 16)
         if i in (2, 4):
@@ -263,71 +267,75 @@
                 for i in which:
                     message_out(g, s, t, i).start()
 
-    def fwd_copies(g):
+    def fwd_rows(g):
         rows = pl.multiple_of((SUB - MARGIN) * SUB * (1 - row), 128)
-        half = pl.multiple_of(COLS_AT + 128 * (1 - row), 128)
-        return [
-            pltpu.make_async_remote_copy(e_v.at[g, pl.ds(rows, 128)], e_v.at[g, pl.ds(ROWS_AT, 128)],
-                                         sf_sem.at[g, 0], rf_sem.at[g, 0], device_id=partner, device_id_type=MESH),
-            pltpu.make_async_remote_copy(e_v.at[g, pl.ds(half, 128)], e_v.at[g, pl.ds(CORN_AT, 128)],
-                                         sf_sem.at[g, 1], rf_sem.at[g, 1], device_id=partner, device_id_type=MESH)]
+        return pltpu.make_async_remote_copy(e_v.at[g, pl.ds(rows, 128)], e_v.at[g, pl.ds(ROWS_AT, 128)],
+                                            sf_sem.at[g, 0], rf_sem.at[g, 0], device_id=partner, device_id_type=MESH)
+
+    def fwd_corners(g):
+        rows = pl.multiple_of(COLS_AT + HALF_COLS * closer, 32)
+        return pltpu.make_async_remote_copy(e_v.at[g, pl.ds(rows, HALF_COLS)], e_v.at[g, pl.ds(CORN_AT, HALF_COLS)],
+                                            sf_sem.at[g, 1], rf_sem.at[g, 1], device_id=partner, device_id_type=MESH)
 
     def assemble(g, sent, first):
         slot = mod(sent, 2)
-        for s in range(2):
-            @pl.when(has[s])
-            def _():
-                for i in FIRST_PARTS if first else SWEEP_PARTS:
-                    message(g, 1 - s, sent, i).wait_recv()
-                for t in range(TILES):
-                    k = g * TILES + t
-                    lanes = pl.ds(t * LANES, LANES)
-                    if first:
-                        theirs = recv_u[slot, g, s, :, lanes]
-                    else:
-                        theirs = recv_b[slot, g, s, pl.ds(0, SUB), lanes].astype(F32)
-                    cells = edge_cells(edge_col[s])
-                    coeff = cedge[s] if first else cedge_om[s]
-                    flux = coeff * (zf[k, edge_cells(edge_col[s], PAD), :] - theirs)
-                    res[k, cells, :] = res[k, cells, :] - flux
-                    halo = (recv_p[slot, g, s, :, lanes] + flux).astype(BF16)
-                    for h in range(2):
-                        at = COLS_AT + 128 * h + 64 * s
-                        e_v[g, pl.ds(at, 16), lanes] = halo[16 * h:16 * h + 16]
-                        e_v[g, pl.ds(at + 16, 48), lanes] = recv_b[slot, g, s, pl.ds(SUB + 48 * h, 48), lanes]
-
-        def pack(rows):
+        for half, parts in ((closer, ((5 if first else 0), 1, 2)), (far, (3, 4))):
+            for s in range(2):
+                @pl.when(has[s])
+                def _():
+                    for i in parts:
+                        message(g, 1 - s, sent, i).wait_recv()
+                    rows = pl.ds(pl.multiple_of(16 * half, 16), 16)
+                    e_rows = pl.ds(pl.multiple_of(SUB + 48 * half, 16), 48)
+                    at = pl.multiple_of(CELLS // 2 * half, CELLS // 2)
+                    e_at = pl.multiple_of(COLS_AT + STEPS * 16 * s + HALF_COLS * half, 16)
+                    cells = pl.ds(at + edge_col[s], 16, stride=SUB)
+                    zcells = pl.ds(PAD + at + edge_col[s], 16, stride=SUB)
+                    coeff = (cedge if first else cedge_om)[s, rows]
+                    for t in range(TILES):
+                        k = g * TILES + t
+                        lanes = pl.ds(t * LANES, LANES)
+                        if first:
+                            theirs = recv_u[slot, g, s, rows, lanes]
+                        else:
+                            theirs = recv_b[slot, g, s, rows, lanes].astype(F32)
+                        flux = coeff * (zf[k, zcells, :] - theirs)
+                        own = res[k, cells, :] - flux
+                        res[k, cells, :] = own
+                        e_v[g, pl.ds(e_at, 16), lanes] = own.astype(BF16)
+                        e_v[g, pl.ds(e_at + 16, 16), lanes] = (recv_p[slot, g, s, rows, lanes] + flux).astype(BF16)
+                        e_v[g, pl.ds(e_at + 32, 48), lanes] = recv_b[slot, g, s, e_rows, lanes]
+            if half is closer:
+                fwd_corners(g).start()
+
+    def pack(g):
+        def one_row(q, carry):
+            rows = pl.ds(pl.multiple_of(q * SUB, SUB), SUB)
             for t in range(TILES):
-                e_v[g, rows, pl.ds(t * LANES, LANES)] = res[g * TILES + t, rows].astype(BF16)
-
-        fwd_rows, fwd_corners = fwd_copies(g)
-        fwd_corners.start()
-        pack(pl.ds(pl.multiple_of((SUB - MARGIN) * SUB * (1 - row), 128), 128))
-        rest = pl.multiple_of(128 * row, 128)
-
-        def pack_rest(q, carry):
-            pack(pl.ds(pl.multiple_of(rest + q * 128, 128), 128))
+                e_v[g, rows, pl.ds(t * LANES, LANES)] = (keep * res[g * TILES + t, rows]).astype(BF16)
             return carry
 
-        fwd_rows.start()
-        lax.fori_loop(0, CELLS // 128 - 1, pack_rest, 0)
-
-    def solve(g):
-        acc[...] = jnp.dot(mat_p[:, :ROWS_AT], e_v[g, pl.ds(0, ROWS_AT)], preferred_element_type=F32)
-        for c in fwd_copies(g):
-            c.wait()
-        acc[...] += jnp.dot(mat_p[:, ROWS_AT:], e_v[g, pl.ds(ROWS_AT, DEPTH - ROWS_AT)], preferred_element_type=F32)
+        lax.fori_loop(0, SUB, one_row, 0, unroll=4)
+        fwd_rows(g).start()
+
+    def solve_own(g):
+        acc[g] = jnp.dot(mat_p[:, :COLS_AT], e_v[g, pl.ds(0, COLS_AT)], preferred_element_type=F32)
+
+    def solve_rest(g):
+        fwd_rows(g).wait()
+        fwd_corners(g).wait()
+        acc[g] += jnp.dot(mat_p[:, COLS_AT:], e_v[g, pl.ds(COLS_AT, DEPTH - COLS_AT)], preferred_element_type=F32)
 
     def round_row(g):
         for t in range(TILES):
-            zrow_s[g, t] = acc[brows, pl.ds(t * LANES, LANES)].astype(BF16).astype(F32)
+            zrow_s[g, t] = acc[g, brows, pl.ds(t * LANES, LANES)].astype(BF16).astype(F32)
 
     def update(g):
         def rows_of(q, carry):
             rows = pl.ds(pl.multiple_of(q * 64, 64), 64)
             for t in range(TILES):
                 k = g * TILES + t
-                z = acc[rows, pl.ds(t * LANES, LANES)].astype(BF16).astype(F32)
+                z = acc[g, rows, pl.ds(t * LANES, LANES)].astype(BF16).astype(F32)
                 zf[k, pl.ds(pl.multiple_of(PAD + q * 64, PAD), 64)] = z
                 u_v[k, rows] = u_v[k, rows] + om * z
             return carry
@@ -338,7 +346,10 @@
         zf[k, pl.ds(0, PAD)] = zero_row
         zf[k, pl.ds(PAD + CELLS, PAD)] = zero_row
     for g in range(groups):
-        e_v[g, pl.ds(COLS_AT, 256)] = jnp.zeros((256, GROUP), BF16)
+        e_v[g, pl.ds(COLS_AT, ROWS_AT - COLS_AT)] = jnp.zeros((ROWS_AT - COLS_AT, GROUP), BF16)
+        e_v[g, pl.ds(CORN_AT, DEPTH - CORN_AT)] = jnp.zeros((DEPTH - CORN_AT, GROUP), BF16)
+    keep = (1.0 - jnp.where(jnp.logical_and(sub_id == 0, has[0]), 1.0, 0.0)
+            - jnp.where(jnp.logical_and(sub_id == SUB - 1, has[1]), 1.0, 0.0))
 
     krow_copy().wait()
     rows_b = pl.ds(pl.multiple_of(PAD + brow * SUB, SUB), SUB)
@@ -346,13 +357,14 @@
 
     def send_bands(g, t):
         stencil_sides(g)
-        fill_half(g, far)
-        start(g, t, (1, 2))
         zrow_copy(g).wait()
         row_fix(g)
         fill_half(g, closer)
+        start(g, t, (1, 2))
+        fill_half(g, far)
         start(g, t, (3, 4))
         stencil_middle(g)
+        pack(g)
 
     for g in range(groups):
         for t in range(TILES):
@@ -380,34 +392,37 @@
             pick = jnp.logical_and(pick, ok(n))
         pick = jnp.where(pick, 1.0, 0.0).astype(BF16)
 
-        acc[...] = jnp.dot(mat_t[:, pl.ds(start, window)], pick, preferred_element_type=F32)
-        mat_p[:, pl.ds(at, width)] = acc[...].astype(BF16)
+        wide[:, pl.ds(0, width)] = jnp.dot(mat_t[:, pl.ds(start, window)], pick, preferred_element_type=F32)
+        mat_p[:, pl.ds(at, width)] = wide[:, pl.ds(0, width)].astype(BF16)
 
     for q in range(4):
         low = (320 * q + 164) // 128 * 128
         high = -(-(320 * q + 476) // 128) * 128
         place(256 * q, 256, low, high - low, lambda n, q=q: own_source(n + 256 * q))
 
-    def side_source(n):
-        r = 16 * (n >> 7) + (n & 15)
-        return (r + MARGIN) * EXT + side_column((n >> 6) & 1, (n >> 4) & 3)
+    for g in range(groups):
+        solve_own(g)
+
+    def column(n):
+        half = n >= HALF_COLS
+        r, c = column_source(jnp.where(half, n - HALF_COLS, n))
+        return (MARGIN + r + jnp.where(half, 16, 0)) * EXT + c
 
     pass_on(1, 0, FIRST_PARTS)
-    place(COLS_AT, 256, 128, 1408, side_source)
-
-    def row_source(n):
-        m = n & 127
+    place(COLS_AT, 384, 128, 1408, column, lambda n: n < 2 * HALF_COLS)
+
+    def halo(n):
         first_row = jnp.where(row == 0, MARGIN + SUB, 0)
-        halo = (first_row + (m >> 5)) * EXT + MARGIN + (m & 31)
-        corner_row = jnp.where(row == 0, MARGIN + SUB, -12) + (m & 15)
-        corner = corner_row * EXT + side_column((m >> 6) & 1, (m >> 4) & 3)
-        return jnp.where(n < 128, halo, corner)
-
-    def row_ok(n):
-        r16 = n & 15
-        return jnp.logical_or(n < 128, jnp.where(row == 0, r16, 15 - r16) < MARGIN)
-
-    place(ROWS_AT, 256, pl.multiple_of(1408 * (1 - row), 128), 192, row_source, row_ok)
+        r, c = column_source(n - 128)
+        corner_row = jnp.where(row == 0, MARGIN + SUB, -12) + r
+        return jnp.where(n < 128, (first_row + (n >> 5)) * EXT + MARGIN + (n & 31), corner_row * EXT + c)
+
+    def halo_ok(n):
+        r = n & 15
+        corner = jnp.logical_and(n < 128 + HALF_COLS, jnp.where(row == 0, r, 15 - r) < MARGIN)
+        return jnp.logical_or(n < 128, corner)
+
+    place(ROWS_AT, 384, pl.multiple_of(1408 * (1 - row), 128), 192, halo, halo_ok)
 
     for s in range(2):
         @pl.when(has[s])
@@ -441,7 +456,7 @@
                 message_on(g, 0, i).wait_send()
 
     def advance(g, t, first, relay):
-        solve(g)
+        solve_rest(g)
         round_row(g)
         zrow_copy(g).start()
         update(g)
@@ -451,6 +466,7 @@
         if relay is not None:
             pass_on(*relay)
         send_bands(g, t)
+        solve_own(g)
 
     assemble(0, 0, True)
     advance(0, 1, True, None)
@@ -475,8 +491,8 @@
             u_copies[g * TILES + t].start()
     for g in range(groups):
         assemble(g, SWEEPS - 1, False)
-        solve(g)
-        z_v[g] = acc[...].astype(BF16)
+        solve_rest(g)
+        z_v[g] = acc[g].astype(BF16)
         z_copies[g].start()
         if g == 0:
             pass_on(1, SWEEPS - 1, SWEEP_PARTS)
@@ -508,7 +524,8 @@
                 vm((EXT * EXT, CELLS), BF16),
                 vm((CELLS, EXT * EXT), BF16),
                 vm((CELLS, DEPTH), BF16),
-                vm((CELLS, GROUP), F32),
+                vm((CELLS, 384), F32),
+                vm((groups, CELLS, GROUP), F32),
                 vm((tiles, CELLS, LANES), F32),
                 vm((tiles, CELLS + 2 * PAD, LANES), F32),
                 vm((tiles, CELLS, LANES), F32),

time: 65.6 us -> 71 us (1.082)
  Pallas kernels: 62.3 us -> 67.7 us
    pallas_call x1, Pallas kernels: 62.3 us -> 67.7 us  [device_fn(): pl.pallas_call(functools.partial(kernel, groups, col_count), out_shape=(j...]
where the time goes in v5:
time: 71 us; the launch traced here: 70.8 us
  Pallas kernels  67.7 us (95%)
  other arithmetic  1.66 us (2%)
  local copies, waits for them, and re-layouts  0.71 us (1%)
    pallas_call x1, Pallas kernels, device_fn(): pl.pallas_call(functools.partial(kernel, groups, col_count), out_shape=(j...  67.7 us
    add x1, other arithmetic, device_fn(): u_last + omega_relax * z_last.astype(F32)  1.66 us

profile of v5, /device:TPU:0, one launch (start us, length us, event | category | flops | bytes accessed | tf_op | source)
XLA Modules:
  0.0 70.8 jit_solution(5625011520765823830)
XLA Ops:
  0.7 0.0 copy-start
  0.7 0.7 %copy-done = f32[32,32]{1,0:T(8,128)S(1)} copy-done((f32[32,32]{1,0:T(8,128)S(1)}, f32[32,32]{1,0:T(8,128)}, u32[]{:S(2)}) %copy-start) | copy-done | bytes 4120
  1.4 67.7 %shard_map.55 = (f32[1024,512]{1,0:T(8,128)S(1)}, bf16[1024,512]{1,0:T(8,128)(2,1)S(1)}) custom-call(f32[1024,512]{1,0:T(8,128)} %bitcast.9, f32[1024,512]{1,0:T(8,128)} %bitcast.10, f32[32,32]{1,0:T(8,128)S(1)} %copy-done, bf16[1600,1024]{1,0:T(8,128)(2,1)} %bitcast.8, f32[1]{0:T(128)} %bitcast.7.om_ref), custom_call_target="tpu_custom_call" | custom-call | tf_op jit(solution)/shard_map/pallas_call | solution.py:516
  69.1 1.7 %multiply_add_fusion = f32[1024,512]{1,0:T(8,128)} fusion(f32[1024,512]{1,0:T(8,128)S(1)} %get-tuple-element.7, bf16[1024,512]{1,0:T(8,128)(2,1)S(1)} %get-tuple-element.8, f32[]{:T(128)} %copy.6), kind=kLoop, calls=%fused_computation | loop fusion | flops 1572864 | bytes 5242884 | tf_op jit(solution)/shard_map/add | solution.py:564
Async XLA Ops:
  0.7 0.7 %copy-start = (f32[32,32]{1,0:T(8,128)S(1)}, f32[32,32]{1,0:T(8,128)}, u32[]{:S(2)}) copy-start(f32[32,32]{1,0:T(8,128)} %kap_ref.1) | copy-start | bytes 12292

commit v6 on v5

--- a/solution.py
+++ b/solution.py
@@ -166,10 +166,10 @@
         lax.fori_loop(0, SUB, one_row, 0, unroll=unroll)
 
     def stencil_sides(g):
-        stencil(g, (0, SUB - 8), (8, 8), 4)
+        stencil(g, (0, SUB - 8), (8, 8), 8)
 
     def stencil_middle(g):
-        stencil(g, (8,), (16,), 4)
+        stencil(g, (8,), (16,), 8)
 
     def zrow_copy(g):
         return pltpu.make_async_remote_copy(
@@ -256,13 +256,13 @@
                         send_b[g, s, pl.ds(e_at + 16 * (d - 1), 16), lanes] = part.astype(BF16)
 
     def start(g, t, which):
-        for s in range(2):
-            @pl.when(jnp.logical_and(has[s], jnp.logical_not(detour[s])))
+        for s, turn in ((1, col < 2), (0, has[0]), (1, jnp.logical_and(col >= 2, has[1]))):
+            @pl.when(jnp.logical_and(turn, jnp.logical_not(detour[s])))
             def _():
                 for i in which:
                     message(g, s, t, i).start()
 
-            @pl.when(detour[s])
+            @pl.when(jnp.logical_and(turn, detour[s]))
             def _():
                 for i in which:
                     message_out(g, s, t, i).start()
@@ -277,36 +277,40 @@
         return pltpu.make_async_remote_copy(e_v.at[g, pl.ds(rows, HALF_COLS)], e_v.at[g, pl.ds(CORN_AT, HALF_COLS)],
                                             sf_sem.at[g, 1], rf_sem.at[g, 1], device_id=partner, device_id_type=MESH)
 
-    def assemble(g, sent, first):
+    def assemble(g, sent, first, half, parts):
         slot = mod(sent, 2)
-        for half, parts in ((closer, ((5 if first else 0), 1, 2)), (far, (3, 4))):
-            for s in range(2):
-                @pl.when(has[s])
-                def _():
-                    for i in parts:
-                        message(g, 1 - s, sent, i).wait_recv()
-                    rows = pl.ds(pl.multiple_of(16 * half, 16), 16)
-                    e_rows = pl.ds(pl.multiple_of(SUB + 48 * half, 16), 48)
-                    at = pl.multiple_of(CELLS // 2 * half, CELLS // 2)
-                    e_at = pl.multiple_of(COLS_AT + STEPS * 16 * s + HALF_COLS * half, 16)
-                    cells = pl.ds(at + edge_col[s], 16, stride=SUB)
-                    zcells = pl.ds(PAD + at + edge_col[s], 16, stride=SUB)
-                    coeff = (cedge if first else cedge_om)[s, rows]
-                    for t in range(TILES):
-                        k = g * TILES + t
-                        lanes = pl.ds(t * LANES, LANES)
-                        if first:
-                            theirs = recv_u[slot, g, s, rows, lanes]
-                        else:
-                            theirs = recv_b[slot, g, s, rows, lanes].astype(F32)
-                        flux = coeff * (zf[k, zcells, :] - theirs)
-                        own = res[k, cells, :] - flux
-                        res[k, cells, :] = own
-                        e_v[g, pl.ds(e_at, 16), lanes] = own.astype(BF16)
-                        e_v[g, pl.ds(e_at + 16, 16), lanes] = (recv_p[slot, g, s, rows, lanes] + flux).astype(BF16)
-                        e_v[g, pl.ds(e_at + 32, 48), lanes] = recv_b[slot, g, s, e_rows, lanes]
-            if half is closer:
-                fwd_corners(g).start()
+        for s in range(2):
+            @pl.when(has[s])
+            def _():
+                for i in parts:
+                    message(g, 1 - s, sent, i).wait_recv()
+                rows = pl.ds(pl.multiple_of(16 * half, 16), 16)
+                e_rows = pl.ds(pl.multiple_of(SUB + 48 * half, 16), 48)
+                at = pl.multiple_of(CELLS // 2 * half, CELLS // 2)
+                e_at = pl.multiple_of(COLS_AT + STEPS * 16 * s + HALF_COLS * half, 16)
+                cells = pl.ds(at + edge_col[s], 16, stride=SUB)
+                zcells = pl.ds(PAD + at + edge_col[s], 16, stride=SUB)
+                coeff = (cedge if first else cedge_om)[s, rows]
+                for t in range(TILES):
+                    k = g * TILES + t
+                    lanes = pl.ds(t * LANES, LANES)
+                    if first:
+                        theirs = recv_u[slot, g, s, rows, lanes]
+                    else:
+                        theirs = recv_b[slot, g, s, rows, lanes].astype(F32)
+                    flux = coeff * (zf[k, zcells, :] - theirs)
+                    own = res[k, cells, :] - flux
+                    res[k, cells, :] = own
+                    e_v[g, pl.ds(e_at, 16), lanes] = own.astype(BF16)
+                    e_v[g, pl.ds(e_at + 16, 16), lanes] = (recv_p[slot, g, s, rows, lanes] + flux).astype(BF16)
+                    e_v[g, pl.ds(e_at + 32, 48), lanes] = recv_b[slot, g, s, e_rows, lanes]
+
+    def assemble_closer(g, sent, first):
+        assemble(g, sent, first, closer, ((5 if first else 0), 1, 2))
+        fwd_corners(g).start()
+
+    def assemble_far(g, sent, first):
+        assemble(g, sent, first, far, (3, 4))
 
     def pack(g):
         def one_row(q, carry):
@@ -319,7 +323,12 @@
         fwd_rows(g).start()
 
     def solve_own(g):
-        acc[g] = jnp.dot(mat_p[:, :COLS_AT], e_v[g, pl.ds(0, COLS_AT)], preferred_element_type=F32)
+        def rows_of(m, carry):
+            rows = pl.ds(pl.multiple_of(m * (CELLS // 2), CELLS // 2), CELLS // 2)
+            acc[g, rows] = jnp.dot(mat_p[rows, :COLS_AT], e_v[g, pl.ds(0, COLS_AT)], preferred_element_type=F32)
+            return carry
+
+        lax.fori_loop(0, 2, rows_of, 0)
 
     def solve_rest(g):
         fwd_rows(g).wait()
@@ -337,7 +346,6 @@
                 k = g * TILES + t
                 z = acc[g, rows, pl.ds(t * LANES, LANES)].astype(BF16).astype(F32)
                 zf[k, pl.ds(pl.multiple_of(PAD + q * 64, PAD), 64)] = z
-                u_v[k, rows] = u_v[k, rows] + om * z
             return carry
 
         lax.fori_loop(0, CELLS // 64, rows_of, 0)
@@ -363,8 +371,6 @@
         start(g, t, (1, 2))
         fill_half(g, far)
         start(g, t, (3, 4))
-        stencil_middle(g)
-        pack(g)
 
     for g in range(groups):
         for t in range(TILES):
@@ -401,6 +407,8 @@
         place(256 * q, 256, low, high - low, lambda n, q=q: own_source(n + 256 * q))
 
     for g in range(groups):
+        stencil_middle(g)
+        pack(g)
         solve_own(g)
 
     def column(n):
@@ -455,7 +463,23 @@
             for i in which:
                 message_on(g, 0, i).wait_send()
 
+    def finish(g):
+        stencil_middle(g)
+        pack(g)
+
+        def add_to_u(q, carry):
+            rows = pl.ds(pl.multiple_of(q * SUB, SUB), SUB)
+            for t in range(TILES):
+                k = g * TILES + t
+                u_v[k, rows] = u_v[k, rows] + om * zf[k, pl.ds(pl.multiple_of(PAD + q * SUB, PAD), SUB)]
+            return carry
+
+        lax.fori_loop(0, SUB, add_to_u, 0, unroll=4)
+        solve_own(g)
+
     def advance(g, t, first, relay):
+        if relay is not None:
+            pass_on(relay[0], relay[1], (0, 1, 2))
         solve_rest(g)
         round_row(g)
         zrow_copy(g).start()
@@ -464,20 +488,24 @@
         fill_z(g, False)
         start(g, t, (0,))
         if relay is not None:
-            pass_on(*relay)
+            pass_on(relay[0], relay[1], (3, 4))
         send_bands(g, t)
-        solve_own(g)
-
-    assemble(0, 0, True)
+
+    assemble_closer(0, 0, True)
+    assemble_far(0, 0, True)
     advance(0, 1, True, None)
-    assemble(1, 0, True)
-    advance(1, 1, True, (0, 1, SWEEP_PARTS))
+    assemble_closer(1, 0, True)
+    finish(0)
+    assemble_far(1, 0, True)
+    advance(1, 1, True, (0, 1))
 
     def step(i, carry):
         t = i // groups
         g = lax.rem(i, groups)
-        assemble(g, t - 1, False)
-        advance(g, t, False, (1 - g, jnp.where(g == 0, t - 1, t), SWEEP_PARTS))
+        assemble_closer(g, t - 1, False)
+        finish(1 - g)
+        assemble_far(g, t - 1, False)
+        advance(g, t, False, (1 - g, jnp.where(g == 0, t - 1, t)))
         return carry
 
     lax.fori_loop(2 * groups, SWEEPS * groups, step, 0)
@@ -488,14 +516,21 @@
                 for g in range(groups)]
     for g in range(groups):
         for t in range(TILES):
-            u_copies[g * TILES + t].start()
-    for g in range(groups):
-        assemble(g, SWEEPS - 1, False)
+            if g == 0:
+                u_copies[t].start()
+        assemble_closer(g, SWEEPS - 1, False)
+        if g == 0:
+            finish(1)
+            for t in range(TILES):
+                u_copies[TILES + t].start()
+        assemble_far(g, SWEEPS - 1, False)
+        if g == 0:
+            pass_on(1, SWEEPS - 1, (0, 1, 2))
         solve_rest(g)
         z_v[g] = acc[g].astype(BF16)
         z_copies[g].start()
         if g == 0:
-            pass_on(1, SWEEPS - 1, SWEEP_PARTS)
+            pass_on(1, SWEEPS - 1, (3, 4))
     for g in range(groups):
         wait_sends(g, SWEEP_PARTS)
     for c in u_copies + z_copies:

time: 71 us -> 63 us (0.89)
  Pallas kernels: 67.7 us -> 59.7 us
    pallas_call x1, Pallas kernels: 67.7 us -> 59.7 us  [device_fn(): pl.pallas_call(functools.partial(kernel, groups, col_count), out_shape=(j...]
where the time goes in v6:
time: 63 us; the launch traced here: 62.8 us
  Pallas kernels  59.7 us (95%)
  other arithmetic  1.66 us (3%)
  local copies, waits for them, and re-layouts  0.71 us (1%)
  between operations  0.67 us (1%)
    pallas_call x1, Pallas kernels, device_fn(): pl.pallas_call(functools.partial(kernel, groups, col_count), out_shape=(j...  59.7 us
    add x1, other arithmetic, device_fn(): u_last + omega_relax * z_last.astype(F32)  1.66 us

profile of v6, /device:TPU:0, one launch (start us, length us, event | category | flops | bytes accessed | tf_op | source)
XLA Modules:
  0.0 62.8 jit_solution(388511061579946401)
XLA Ops:
  0.7 0.0 copy-start
  0.7 0.7 %copy-done = f32[32,32]{1,0:T(8,128)S(1)} copy-done((f32[32,32]{1,0:T(8,128)S(1)}, f32[32,32]{1,0:T(8,128)}, u32[]{:S(2)}) %copy-start) | copy-done | bytes 4120
  1.4 59.7 %shard_map.55 = (f32[1024,512]{1,0:T(8,128)S(1)}, bf16[1024,512]{1,0:T(8,128)(2,1)S(1)}) custom-call(f32[1024,512]{1,0:T(8,128)} %bitcast.9, f32[1024,512]{1,0:T(8,128)} %bitcast.10, f32[32,32]{1,0:T(8,128)S(1)} %copy-done, bf16[1600,1024]{1,0:T(8,128)(2,1)} %bitcast.8, f32[1]{0:T(128)} %bitcast.7.om_ref), custom_call_target="tpu_custom_call" | custom-call | tf_op jit(solution)/shard_map/pallas_call | solution.py:551
  61.1 1.7 %multiply_add_fusion = f32[1024,512]{1,0:T(8,128)} fusion(f32[1024,512]{1,0:T(8,128)S(1)} %get-tuple-element.7, bf16[1024,512]{1,0:T(8,128)(2,1)S(1)} %get-tuple-element.8, f32[]{:T(128)} %copy.6), kind=kLoop, calls=%fused_computation | loop fusion | flops 1572864 | bytes 5242884 | tf_op jit(solution)/shard_map/add | solution.py:599
Async XLA Ops:
  0.7 0.7 %copy-start = (f32[32,32]{1,0:T(8,128)S(1)}, f32[32,32]{1,0:T(8,128)}, u32[]{:S(2)}) copy-start(f32[32,32]{1,0:T(8,128)} %kap_ref.1) | copy-start | bytes 12292

commit v7 on v6

--- a/solution.py
+++ b/solution.py
@@ -42,7 +42,7 @@
 
 def kernel(groups, col_count,
            f_hbm, u_hbm, kap_ref, mat_hbm, om_ref, u_out, z_out,
-           mat_v, mat_t, mat_p, wide, acc, res, zf, u_v, e_v, z_v, kb, cd, cn, cs, cw, ce, cedge, cedge_om, crow,
+           mat_v, mat_t, mat_p, wide, acc, res, zf, u_v, e_v, z_v, kb, coef, cedge, cedge_om, crow,
            send_p, send_b, send_u, recv_p, recv_b, recv_u, zrow_s, zrow, kcol_s, kcol_r, krow_r,
            via_p, via_b, via_u,
            in_sem, mat_sem, out_sem, s_sem, r_sem,
@@ -138,21 +138,20 @@
                                        jnp.logical_and(q == SUB - 1, row == 1)), 1.0, 0.0)
         rim_col = jnp.where(sub_id == 0, no_w, 0.0) + jnp.where(sub_id == SUB - 1, no_e, 0.0)
         rows = pl.ds(base, SUB)
-        cn[rows] = vn
-        cs[rows] = vs
-        cw[rows] = vw
-        ce[rows] = ve
-        cd[rows] = vn + vs + vw + ve + (rim + rim_col) * here
+        vd = vn + vs + vw + ve + (rim + rim_col) * here
+        for j, v in enumerate((vd, vn, vs, vw, ve)):
+            coef[0, j, rows] = v
+            coef[1, j, rows] = om * v
         return carry
 
     lax.fori_loop(0, SUB, coeff_row, 0)
 
-    def stencil(g, first, count, unroll):
+    def stencil(g, scaled, first, count, unroll):
         def one_row(q, carry):
             for at, n in zip(first, count):
                 base = pl.multiple_of(q * SUB + at, 8)
                 rows = pl.ds(base, n)
-                vd, vn, vs, vw, ve = cd[rows], cn[rows], cs[rows], cw[rows], ce[rows]
+                vd, vn, vs, vw, ve = (coef[scaled, j, rows] for j in range(5))
                 for t in range(TILES):
                     k = g * TILES + t
                     part = (vd * zf[k, pl.ds(PAD + base, n)]
@@ -165,11 +164,11 @@
 
         lax.fori_loop(0, SUB, one_row, 0, unroll=unroll)
 
-    def stencil_sides(g):
-        stencil(g, (0, SUB - 8), (8, 8), 8)
-
-    def stencil_middle(g):
-        stencil(g, (8,), (16,), 8)
+    def stencil_sides(g, scaled):
+        stencil(g, scaled, (0, SUB - 8), (8, 8), 8)
+
+    def stencil_middle(g, scaled):
+        stencil(g, scaled, (8,), (16,), 8)
 
     def zrow_copy(g):
         return pltpu.make_async_remote_copy(
@@ -177,10 +176,10 @@
 
     brows = pl.ds(pl.multiple_of(brow * SUB, SUB), SUB)
 
-    def row_fix(g):
+    def row_fix(g, scaled):
         for t in range(TILES):
             k = g * TILES + t
-            res[k, brows] = res[k, brows] - crow[...] * (zrow_s[g, t] - zrow[g, t])
+            res[k, brows] = res[k, brows] - crow[scaled] * (zrow_s[g, t] - zrow[g, t])
 
     def near(s, dist):
         return dist if s == 0 else SUB - 1 - dist
@@ -361,12 +360,13 @@
 
     krow_copy().wait()
     rows_b = pl.ds(pl.multiple_of(PAD + brow * SUB, SUB), SUB)
-    crow[...] = 0.5 * (kb[rows_b] + krow_r[...])
-
-    def send_bands(g, t):
-        stencil_sides(g)
+    crow[0] = 0.5 * (kb[rows_b] + krow_r[...])
+    crow[1] = om * crow[0]
+
+    def send_bands(g, t, scaled):
+        stencil_sides(g, scaled)
         zrow_copy(g).wait()
-        row_fix(g)
+        row_fix(g, scaled)
         fill_half(g, closer)
         start(g, t, (1, 2))
         fill_half(g, far)
@@ -382,15 +382,29 @@
         start(g, 0, (5,))
         for t in range(TILES):
             loads[g * TILES + t][1].wait()
-        send_bands(g, 0)
+        send_bands(g, 0, 0)
+
+    def finish(g, scaled):
+        stencil_middle(g, scaled)
+        pack(g)
+
+        def add_to_u(q, carry):
+            rows = pl.ds(pl.multiple_of(q * SUB, SUB), SUB)
+            for t in range(TILES):
+                k = g * TILES + t
+                u_v[k, rows] = u_v[k, rows] + om * zf[k, pl.ds(pl.multiple_of(PAD + q * SUB, PAD), SUB)]
+            return carry
+
+        if scaled:
+            lax.fori_loop(0, SUB, add_to_u, 0, unroll=4)
+        solve_own(g)
 
     mat_copy.wait()
     for at in range(0, EXT * EXT, 256):
         span = pl.ds(at, min(256, EXT * EXT - at))
         mat_t[:, span] = mat_v[span].T
-    pass_on(0, 0, FIRST_PARTS)
-
-    def place(at, width, start, window, source, ok=None):
+
+    def place(at, width, start, window, source, ok=None, add=False):
         n = lax.broadcasted_iota(jnp.int32, (window, width), 1)
         k = lax.broadcasted_iota(jnp.int32, (window, width), 0) + start
         pick = source(n) == k
@@ -399,25 +413,32 @@
         pick = jnp.where(pick, 1.0, 0.0).astype(BF16)
 
         wide[:, pl.ds(0, width)] = jnp.dot(mat_t[:, pl.ds(start, window)], pick, preferred_element_type=F32)
-        mat_p[:, pl.ds(at, width)] = wide[:, pl.ds(0, width)].astype(BF16)
+        placed = wide[:, pl.ds(0, width)].astype(BF16)
+        if add:
+            overlap = pl.ds(at, add)
+            mat_p[:, overlap] = mat_p[:, overlap] + placed[:, :add]
+            mat_p[:, pl.ds(at + add, width - add)] = placed[:, add:]
+        else:
+            mat_p[:, pl.ds(at, width)] = placed
 
     for q in range(4):
         low = (320 * q + 164) // 128 * 128
         high = -(-(320 * q + 476) // 128) * 128
         place(256 * q, 256, low, high - low, lambda n, q=q: own_source(n + 256 * q))
 
-    for g in range(groups):
-        stencil_middle(g)
-        pack(g)
-        solve_own(g)
-
-    def column(n):
-        half = n >= HALF_COLS
-        r, c = column_source(jnp.where(half, n - HALF_COLS, n))
-        return (MARGIN + r + jnp.where(half, 16, 0)) * EXT + c
-
+    pass_on(0, 0, FIRST_PARTS)
+    finish(0, 0)
+
+    def column(half):
+        def source(n):
+            r, c = column_source(n + 128 * half - HALF_COLS * half)
+            return (MARGIN + 16 * half + r) * EXT + c
+        return source
+
+    place(COLS_AT, 256, 128, 768, column(0), lambda n: n < HALF_COLS)
+    place(COLS_AT + 128, 256, 768, 768, column(1),
+          lambda n: jnp.logical_and(n >= HALF_COLS - 128, n < 2 * HALF_COLS - 128), add=128)
     pass_on(1, 0, FIRST_PARTS)
-    place(COLS_AT, 384, 128, 1408, column, lambda n: n < 2 * HALF_COLS)
 
     def halo(n):
         first_row = jnp.where(row == 0, MARGIN + SUB, 0)
@@ -439,15 +460,6 @@
             cedge[s] = 0.5 * (kcol_s[s] + kcol_r[s])
             cedge_om[s] = om * cedge[s]
             kcol_copy(s).wait_send()
-    crow[...] = om * crow[...]
-
-    def scale(q, carry):
-        rows = pl.ds(pl.multiple_of(q * SUB, SUB), SUB)
-        for c in (cd, cn, cs, cw, ce):
-            c[rows] = om * c[rows]
-        return carry
-
-    lax.fori_loop(0, SUB, scale, 0)
     for k in range(groups * TILES):
         loads[k][2].wait()
 
@@ -462,20 +474,6 @@
         def _():
             for i in which:
                 message_on(g, 0, i).wait_send()
-
-    def finish(g):
-        stencil_middle(g)
-        pack(g)
-
-        def add_to_u(q, carry):
-            rows = pl.ds(pl.multiple_of(q * SUB, SUB), SUB)
-            for t in range(TILES):
-                k = g * TILES + t
-                u_v[k, rows] = u_v[k, rows] + om * zf[k, pl.ds(pl.multiple_of(PAD + q * SUB, PAD), SUB)]
-            return carry
-
-        lax.fori_loop(0, SUB, add_to_u, 0, unroll=4)
-        solve_own(g)
 
     def advance(g, t, first, relay):
         if relay is not None:
@@ -489,13 +487,14 @@
         start(g, t, (0,))
         if relay is not None:
             pass_on(relay[0], relay[1], (3, 4))
-        send_bands(g, t)
+        send_bands(g, t, 1)
 
     assemble_closer(0, 0, True)
+    finish(1, 0)
     assemble_far(0, 0, True)
     advance(0, 1, True, None)
     assemble_closer(1, 0, True)
-    finish(0)
+    finish(0, 1)
     assemble_far(1, 0, True)
     advance(1, 1, True, (0, 1))
 
@@ -503,7 +502,7 @@
         t = i // groups
         g = lax.rem(i, groups)
         assemble_closer(g, t - 1, False)
-        finish(1 - g)
+        finish(1 - g, 1)
         assemble_far(g, t - 1, False)
         advance(g, t, False, (1 - g, jnp.where(g == 0, t - 1, t)))
         return carry
@@ -520,7 +519,7 @@
                 u_copies[t].start()
         assemble_closer(g, SWEEPS - 1, False)
         if g == 0:
-            finish(1)
+            finish(1, 1)
             for t in range(TILES):
                 u_copies[TILES + t].start()
         assemble_far(g, SWEEPS - 1, False)
@@ -547,7 +546,6 @@
         tiles = rhs_count // LANES
         vm = pltpu.VMEM
         dma = pltpu.SemaphoreType.DMA
-        coeff = vm((CELLS, LANES), F32)
         u_last, z_last = pl.pallas_call(
             functools.partial(kernel, groups, col_count),
             out_shape=(jax.ShapeDtypeStruct((CELLS, rhs_count), F32), jax.ShapeDtypeStruct((CELLS, rhs_count), BF16)),
@@ -567,10 +565,10 @@
                 vm((groups, DEPTH, GROUP), BF16),
                 vm((groups, CELLS, GROUP), BF16),
                 vm((CELLS + 2 * PAD, LANES), F32),
-                coeff, coeff, coeff, coeff, coeff,
+                vm((2, 5, CELLS, LANES), F32),
                 vm((2, SUB, LANES), F32),
                 vm((2, SUB, LANES), F32),
-                vm((SUB, LANES), F32),
+                vm((2, SUB, LANES), F32),
                 vm((groups, 2, SUB, GROUP), F32),
                 vm((groups, 2, 128, GROUP), BF16),
                 vm((groups, 2, SUB, GROUP), F32),

time: 63 us -> 59.8 us (0.949)
  Pallas kernels: 59.7 us -> 56.6 us
    pallas_call x1, Pallas kernels: 59.7 us -> 56.6 us  [device_fn(): pl.pallas_call(functools.partial(kernel, groups, col_count), out_shape=(j...]
where the time goes in v7:
time: 59.8 us; the launch traced here: 59.7 us
  Pallas kernels  56.6 us (95%)
  other arithmetic  1.66 us (3%)
  local copies, waits for them, and re-layouts  0.71 us (1%)
  between operations  0.67 us (1%)
    pallas_call x1, Pallas kernels, device_fn(): pl.pallas_call(functools.partial(kernel, groups, col_count), out_shape=(j...  56.6 us
    add x1, other arithmetic, device_fn(): u_last + omega_relax * z_last.astype(F32)  1.66 us

profile of v7, /device:TPU:0, one launch (start us, length us, event | category | flops | bytes accessed | tf_op | source)
XLA Modules:
  0.0 59.7 jit_solution(10762163269383047594)
XLA Ops:
  0.7 0.0 copy-start
  0.7 0.7 %copy-done = f32[32,32]{1,0:T(8,128)S(1)} copy-done((f32[32,32]{1,0:T(8,128)S(1)}, f32[32,32]{1,0:T(8,128)}, u32[]{:S(2)}) %copy-start) | copy-done | bytes 4120
  1.4 56.6 %shard_map.55 = (f32[1024,512]{1,0:T(8,128)S(1)}, bf16[1024,512]{1,0:T(8,128)(2,1)S(1)}) custom-call(f32[1024,512]{1,0:T(8,128)} %bitcast.9, f32[1024,512]{1,0:T(8,128)} %bitcast.10, f32[32,32]{1,0:T(8,128)S(1)} %copy-done, bf16[1600,1024]{1,0:T(8,128)(2,1)} %bitcast.8, f32[1]{0:T(128)} %bitcast.7.om_ref), custom_call_target="tpu_custom_call" | custom-call | tf_op jit(solution)/shard_map/pallas_call | solution.py:549
  58.0 1.7 %multiply_add_fusion = f32[1024,512]{1,0:T(8,128)} fusion(f32[1024,512]{1,0:T(8,128)S(1)} %get-tuple-element.7, bf16[1024,512]{1,0:T(8,128)(2,1)S(1)} %get-tuple-element.8, f32[]{:T(128)} %copy.6), kind=kLoop, calls=%fused_computation | loop fusion | flops 1572864 | bytes 5242884 | tf_op jit(solution)/shard_map/add | solution.py:597
Async XLA Ops:
  0.7 0.7 %copy-start = (f32[32,32]{1,0:T(8,128)S(1)}, f32[32,32]{1,0:T(8,128)}, u32[]{:S(2)}) copy-start(f32[32,32]{1,0:T(8,128)} %kap_ref.1) | copy-start | bytes 12292

commit v8 on v7

--- a/solution.py
+++ b/solution.py
@@ -146,29 +146,22 @@
 
     lax.fori_loop(0, SUB, coeff_row, 0)
 
-    def stencil(g, scaled, first, count, unroll):
+    def stencil(g, scaled):
         def one_row(q, carry):
-            for at, n in zip(first, count):
-                base = pl.multiple_of(q * SUB + at, 8)
-                rows = pl.ds(base, n)
-                vd, vn, vs, vw, ve = (coef[scaled, j, rows] for j in range(5))
-                for t in range(TILES):
-                    k = g * TILES + t
-                    part = (vd * zf[k, pl.ds(PAD + base, n)]
-                            - vn * zf[k, pl.ds(base, n)]
-                            - vs * zf[k, pl.ds(2 * PAD + base, n)]
-                            - vw * zf[k, pl.ds(PAD - 1 + base, n)]
-                            - ve * zf[k, pl.ds(PAD + 1 + base, n)])
-                    res[k, rows] = res[k, rows] - part
+            base = pl.multiple_of(q * SUB, SUB)
+            rows = pl.ds(base, SUB)
+            vd, vn, vs, vw, ve = (coef[scaled, j, rows] for j in range(5))
+            for t in range(TILES):
+                k = g * TILES + t
+                part = (vd * zf[k, pl.ds(PAD + base, SUB)]
+                        - vn * zf[k, pl.ds(base, SUB)]
+                        - vs * zf[k, pl.ds(2 * PAD + base, SUB)]
+                        - vw * zf[k, pl.ds(PAD - 1 + base, SUB)]
+                        - ve * zf[k, pl.ds(PAD + 1 + base, SUB)])
+                res[k, rows] = res[k, rows] - part
             return carry
 
-        lax.fori_loop(0, SUB, one_row, 0, unroll=unroll)
-
-    def stencil_sides(g, scaled):
-        stencil(g, scaled, (0, SUB - 8), (8, 8), 8)
-
-    def stencil_middle(g, scaled):
-        stencil(g, scaled, (8,), (16,), 8)
+        lax.fori_loop(0, SUB, one_row, 0, unroll=4)
 
     def zrow_copy(g):
         return pltpu.make_async_remote_copy(
@@ -311,11 +304,14 @@
     def assemble_far(g, sent, first):
         assemble(g, sent, first, far, (3, 4))
 
-    def pack(g):
+    def pack(g, scaled):
         def one_row(q, carry):
             rows = pl.ds(pl.multiple_of(q * SUB, SUB), SUB)
             for t in range(TILES):
-                e_v[g, rows, pl.ds(t * LANES, LANES)] = (keep * res[g * TILES + t, rows]).astype(BF16)
+                k = g * TILES + t
+                e_v[g, rows, pl.ds(t * LANES, LANES)] = (keep * res[k, rows]).astype(BF16)
+                if scaled:
+                    u_v[k, rows] = u_v[k, rows] + om * zf[k, pl.ds(pl.multiple_of(PAD + q * SUB, PAD), SUB)]
             return carry
 
         lax.fori_loop(0, SUB, one_row, 0, unroll=4)
@@ -364,7 +360,7 @@
     crow[1] = om * crow[0]
 
     def send_bands(g, t, scaled):
-        stencil_sides(g, scaled)
+        stencil(g, scaled)
         zrow_copy(g).wait()
         row_fix(g, scaled)
         fill_half(g, closer)
@@ -385,18 +381,7 @@
         send_bands(g, 0, 0)
 
     def finish(g, scaled):
-        stencil_middle(g, scaled)
-        pack(g)
-
-        def add_to_u(q, carry):
-            rows = pl.ds(pl.multiple_of(q * SUB, SUB), SUB)
-            for t in range(TILES):
-                k = g * TILES + t
-                u_v[k, rows] = u_v[k, rows] + om * zf[k, pl.ds(pl.multiple_of(PAD + q * SUB, PAD), SUB)]
-            return carry
-
-        if scaled:
-            lax.fori_loop(0, SUB, add_to_u, 0, unroll=4)
+        pack(g, scaled)
         solve_own(g)
 
     mat_copy.wait()

time: 59.8 us -> 58.6 us (0.980)
  Pallas kernels: 56.6 us -> 55.3 us
    pallas_call x1, Pallas kernels: 56.6 us -> 55.3 us  [device_fn(): pl.pallas_call(functools.partial(kernel, groups, col_count), out_shape=(j...]
where the time goes in v8:
time: 58.6 us; the launch traced here: 58.4 us
  Pallas kernels  55.3 us (94%)
  other arithmetic  1.66 us (3%)
  local copies, waits for them, and re-layouts  0.71 us (1%)
  between operations  0.67 us (1%)
    pallas_call x1, Pallas kernels, device_fn(): pl.pallas_call(functools.partial(kernel, groups, col_count), out_shape=(j...  55.3 us
    add x1, other arithmetic, device_fn(): u_last + omega_relax * z_last.astype(F32)  1.66 us

profile of v8, /device:TPU:0, one launch (start us, length us, event | category | flops | bytes accessed | tf_op | source)
XLA Modules:
  0.0 58.4 jit_solution(11000315512720685816)
XLA Ops:
  0.7 0.0 copy-start
  0.7 0.7 %copy-done = f32[32,32]{1,0:T(8,128)S(1)} copy-done((f32[32,32]{1,0:T(8,128)S(1)}, f32[32,32]{1,0:T(8,128)}, u32[]{:S(2)}) %copy-start) | copy-done | bytes 4120
  1.4 55.3 %shard_map.55 = (f32[1024,512]{1,0:T(8,128)S(1)}, bf16[1024,512]{1,0:T(8,128)(2,1)S(1)}) custom-call(f32[1024,512]{1,0:T(8,128)} %bitcast.9, f32[1024,512]{1,0:T(8,128)} %bitcast.10, f32[32,32]{1,0:T(8,128)S(1)} %copy-done, bf16[1600,1024]{1,0:T(8,128)(2,1)} %bitcast.8, f32[1]{0:T(128)} %bitcast.7.om_ref), custom_call_target="tpu_custom_call" | custom-call | tf_op jit(solution)/shard_map/pallas_call | solution.py:534
  56.7 1.7 %multiply_add_fusion = f32[1024,512]{1,0:T(8,128)} fusion(f32[1024,512]{1,0:T(8,128)S(1)} %get-tuple-element.7, bf16[1024,512]{1,0:T(8,128)(2,1)S(1)} %get-tuple-element.8, f32[]{:T(128)} %copy.6), kind=kLoop, calls=%fused_computation | loop fusion | flops 1572864 | bytes 5242884 | tf_op jit(solution)/shard_map/add | solution.py:582
Async XLA Ops:
  0.7 0.7 %copy-start = (f32[32,32]{1,0:T(8,128)S(1)}, f32[32,32]{1,0:T(8,128)}, u32[]{:S(2)}) copy-start(f32[32,32]{1,0:T(8,128)} %kap_ref.1) | copy-start | bytes 12292

commit v9 on v8

--- a/solution.py
+++ b/solution.py
@@ -69,15 +69,12 @@
             lanes = pl.ds(k * LANES, LANES)
             loads.append((
                 pltpu.make_async_copy(u_hbm.at[:, lanes], zf.at[k, pl.ds(PAD, CELLS)], in_sem.at[0, k]),
-                pltpu.make_async_copy(f_hbm.at[:, lanes], res.at[k], in_sem.at[1, k]),
-                pltpu.make_async_copy(u_hbm.at[:, lanes], u_v.at[k], in_sem.at[2, k])))
-    for a, b, c in loads:
-        a.start()
-        b.start()
+                pltpu.make_async_copy(f_hbm.at[:, lanes], res.at[k], in_sem.at[1, k])))
     mat_copy = pltpu.make_async_copy(mat_hbm, mat_v, mat_sem)
-    mat_copy.start()
-    for a, b, c in loads:
-        c.start()
+    for t in range(TILES):
+        loads[t][0].start()
+    for t in range(TILES):
+        loads[t][1].start()
 
     barrier = pltpu.get_barrier_semaphore()
     pl.semaphore_signal(barrier, inc=1, device_id=partner, device_id_type=MESH)
@@ -180,16 +177,12 @@
     far = row
     closer = 1 - row
 
-    def part(g, i):
-        half = (closer, far)[(i - 1) // 2 % 2]
-        if i in (1, 3):
-            return 1, pl.ds(pl.multiple_of(16 * half, 16), 16)
-        if i in (2, 4):
-            return 0, pl.ds(pl.multiple_of(SUB + 48 * half, 16), 48)
-        return (0 if i == 0 else 2), pl.ds(0, SUB)
+    def part(i):
+        return {0: (0, pl.ds(0, SUB)), 1: (1, pl.ds(0, 16)), 2: (0, pl.ds(SUB, 48)), 3: (1, pl.ds(16, 16)),
+                4: (0, pl.ds(80, 48)), 5: (2, pl.ds(0, SUB))}[i]
 
     def message(g, s, t, i):
-        kind, rows = part(g, i)
+        kind, rows = part(i)
         slot = mod(t, 2)
         src = (send_b, send_p, send_u)[kind].at[g, s, rows]
         dst = (recv_b, recv_p, recv_u)[kind].at[slot, g, 1 - s, rows]
@@ -197,7 +190,7 @@
                                             device_id=side_dev[s], device_id_type=MESH)
 
     def message_out(g, s, t, i):
-        kind, rows = part(g, i)
+        kind, rows = part(i)
         slot = mod(t, 3)
         src = (send_b, send_p, send_u)[kind].at[g, s, rows]
         dst = (via_b, via_p, via_u)[kind].at[slot, g, rows]
@@ -205,15 +198,15 @@
                                             device_id=mate, device_id_type=MESH)
 
     def message_on(g, t, i):
-        kind, rows = part(g, i)
+        kind, rows = part(i)
         slot = mod(t, 2)
         src = (via_b, via_p, via_u)[kind].at[mod(t, 3), g, rows]
         dst = (recv_b, recv_p, recv_u)[kind].at[slot, g, via_side, rows]
         return pltpu.make_async_remote_copy(src, dst, vs_sem.at[g, i], r_sem.at[slot, g, via_side, i],
                                             device_id=via_to, device_id_type=MESH)
 
-    SWEEP_PARTS = (0, 1, 2, 3, 4)
-    FIRST_PARTS = (5, 1, 2, 3, 4)
+    SWEEP_PARTS = (0, 2, 1, 4, 3)
+    FIRST_PARTS = (5, 2, 1, 4, 3)
 
     def pass_on(g, t, parts):
         @pl.when(is_via)
@@ -222,30 +215,32 @@
                 message_out(g, 0, t, i).wait_recv()
                 message_on(g, t, i).start()
 
-    def fill_z(g, first):
+    def fill_u(g):
         for s in range(2):
             for t in range(TILES):
-                lanes = pl.ds(t * LANES, LANES)
-                zedge = zf[g * TILES + t, edge_cells(near(s, 0), PAD), :]
-                if first:
-                    send_u[g, s, :, lanes] = zedge
-                else:
-                    send_b[g, s, pl.ds(0, SUB), lanes] = zedge.astype(BF16)
+                send_u[g, s, :, pl.ds(t * LANES, LANES)] = zf[g * TILES + t, edge_cells(near(s, 0), PAD), :]
+
+    def fill_z(g):
+        for j, h in enumerate((closer, far)):
+            at = pl.multiple_of(CELLS // 2 * h, CELLS // 2)
+            for s in range(2):
+                for t in range(TILES):
+                    zedge = zf[g * TILES + t, pl.ds(PAD + at + near(s, 0), 16, stride=SUB), :]
+                    send_b[g, s, pl.ds(16 * j, 16), pl.ds(t * LANES, LANES)] = zedge.astype(BF16)
 
     def fill_half(g, h):
         at = pl.multiple_of(CELLS // 2 * h, CELLS // 2)
-        p_at = pl.multiple_of(16 * h, 16)
-        e_at = pl.multiple_of(SUB + 48 * h, 16)
+        j = 0 if h is closer else 1
         for s in range(2):
             for t in range(TILES):
                 k = g * TILES + t
                 lanes = pl.ds(t * LANES, LANES)
                 for d in range(MARGIN):
-                    part = res[k, pl.ds(at + near(s, d), 16, stride=SUB), :]
+                    band = res[k, pl.ds(at + near(s, d), 16, stride=SUB), :]
                     if d == 0:
-                        send_p[g, s, pl.ds(p_at, 16), lanes] = part
+                        send_p[g, s, pl.ds(16 * j, 16), lanes] = band
                     else:
-                        send_b[g, s, pl.ds(e_at + 16 * (d - 1), 16), lanes] = part.astype(BF16)
+                        send_b[g, s, pl.ds(SUB + 48 * j + 16 * (d - 1), 16), lanes] = band.astype(BF16)
 
     def start(g, t, which):
         for s, turn in ((1, col < 2), (0, has[0]), (1, jnp.logical_and(col >= 2, has[1]))):
@@ -271,13 +266,15 @@
 
     def assemble(g, sent, first, half, parts):
         slot = mod(sent, 2)
+        j = 0 if half is closer else 1
+        j_rows = pl.ds(16 * j, 16)
         for s in range(2):
             @pl.when(has[s])
             def _():
                 for i in parts:
                     message(g, 1 - s, sent, i).wait_recv()
                 rows = pl.ds(pl.multiple_of(16 * half, 16), 16)
-                e_rows = pl.ds(pl.multiple_of(SUB + 48 * half, 16), 48)
+                e_rows = pl.ds(SUB + 48 * j, 48)
                 at = pl.multiple_of(CELLS // 2 * half, CELLS // 2)
                 e_at = pl.multiple_of(COLS_AT + STEPS * 16 * s + HALF_COLS * half, 16)
                 cells = pl.ds(at + edge_col[s], 16, stride=SUB)
@@ -289,20 +286,20 @@
                     if first:
                         theirs = recv_u[slot, g, s, rows, lanes]
                     else:
-                        theirs = recv_b[slot, g, s, rows, lanes].astype(F32)
+                        theirs = recv_b[slot, g, s, j_rows, lanes].astype(F32)
                     flux = coeff * (zf[k, zcells, :] - theirs)
                     own = res[k, cells, :] - flux
                     res[k, cells, :] = own
                     e_v[g, pl.ds(e_at, 16), lanes] = own.astype(BF16)
-                    e_v[g, pl.ds(e_at + 16, 16), lanes] = (recv_p[slot, g, s, rows, lanes] + flux).astype(BF16)
+                    e_v[g, pl.ds(e_at + 16, 16), lanes] = (recv_p[slot, g, s, j_rows, lanes] + flux).astype(BF16)
                     e_v[g, pl.ds(e_at + 32, 48), lanes] = recv_b[slot, g, s, e_rows, lanes]
 
     def assemble_closer(g, sent, first):
-        assemble(g, sent, first, closer, ((5 if first else 0), 1, 2))
+        assemble(g, sent, first, closer, (5 if first else 0, 2, 1))
         fwd_corners(g).start()
 
     def assemble_far(g, sent, first):
-        assemble(g, sent, first, far, (3, 4))
+        assemble(g, sent, first, far, (4, 3))
 
     def pack(g, scaled):
         def one_row(q, carry):
@@ -310,8 +307,8 @@
             for t in range(TILES):
                 k = g * TILES + t
                 e_v[g, rows, pl.ds(t * LANES, LANES)] = (keep * res[k, rows]).astype(BF16)
-                if scaled:
-                    u_v[k, rows] = u_v[k, rows] + om * zf[k, pl.ds(pl.multiple_of(PAD + q * SUB, PAD), SUB)]
+                z = zf[k, pl.ds(pl.multiple_of(PAD + q * SUB, PAD), SUB)]
+                u_v[k, rows] = u_v[k, rows] + om * z if scaled else z
             return carry
 
         lax.fori_loop(0, SUB, one_row, 0, unroll=4)
@@ -364,9 +361,9 @@
         zrow_copy(g).wait()
         row_fix(g, scaled)
         fill_half(g, closer)
-        start(g, t, (1, 2))
+        start(g, t, (2, 1))
         fill_half(g, far)
-        start(g, t, (3, 4))
+        start(g, t, (4, 3))
 
     for g in range(groups):
         for t in range(TILES):
@@ -374,10 +371,15 @@
         for t in range(TILES):
             zrow_s[g, t] = zf[g * TILES + t, rows_b]
         zrow_copy(g).start()
-        fill_z(g, True)
+        fill_u(g)
         start(g, 0, (5,))
         for t in range(TILES):
             loads[g * TILES + t][1].wait()
+        if g == 0:
+            for a, b in loads[TILES:]:
+                a.start()
+                b.start()
+            mat_copy.start()
         send_bands(g, 0, 0)
 
     def finish(g, scaled):
@@ -445,8 +447,6 @@
             cedge[s] = 0.5 * (kcol_s[s] + kcol_r[s])
             cedge_om[s] = om * cedge[s]
             kcol_copy(s).wait_send()
-    for k in range(groups * TILES):
-        loads[k][2].wait()
 
     def wait_sends(g, which):
         for s in range(2):
@@ -462,16 +462,16 @@
 
     def advance(g, t, first, relay):
         if relay is not None:
-            pass_on(relay[0], relay[1], (0, 1, 2))
+            pass_on(relay[0], relay[1], (0, 2, 1))
         solve_rest(g)
         round_row(g)
         zrow_copy(g).start()
         update(g)
         wait_sends(g, FIRST_PARTS if first else SWEEP_PARTS)
-        fill_z(g, False)
+        fill_z(g)
         start(g, t, (0,))
         if relay is not None:
-            pass_on(relay[0], relay[1], (3, 4))
+            pass_on(relay[0], relay[1], (4, 3))
         send_bands(g, t, 1)
 
     assemble_closer(0, 0, True)
@@ -509,12 +509,12 @@
                 u_copies[TILES + t].start()
         assemble_far(g, SWEEPS - 1, False)
         if g == 0:
-            pass_on(1, SWEEPS - 1, (0, 1, 2))
+            pass_on(1, SWEEPS - 1, (0, 2, 1))
         solve_rest(g)
         z_v[g] = acc[g].astype(BF16)
         z_copies[g].start()
         if g == 0:
-            pass_on(1, SWEEPS - 1, (3, 4))
+            pass_on(1, SWEEPS - 1, (4, 3))
     for g in range(groups):
         wait_sends(g, SWEEP_PARTS)
     for c in u_copies + z_copies:
@@ -568,7 +568,7 @@
                 vm((3, groups, SUB, GROUP), F32),
                 vm((3, groups, 128, GROUP), BF16),
                 vm((1, groups, SUB, GROUP), F32),
-                dma((3, tiles)), dma, dma((groups,)),
+                dma((2, tiles)), dma, dma((groups,)),
                 dma((groups, 2, 6)), dma((2, groups, 2, 6)),
                 dma((groups,)), dma((groups,)),
                 dma((groups, 2)), dma((groups, 2)),

time: 58.6 us -> 58.3 us (level)
  no operation moved by 1% of the time
where the time goes in v9:
time: 58.3 us; the launch traced here: 58.1 us
  Pallas kernels  55.1 us (95%)
  other arithmetic  1.66 us (3%)
  local copies, waits for them, and re-layouts  0.71 us (1%)
  between operations  0.67 us (1%)
    pallas_call x1, Pallas kernels, device_fn(): pl.pallas_call(functools.partial(kernel, groups, col_count), out_shape=(j...  55.1 us
    add x1, other arithmetic, device_fn(): u_last + omega_relax * z_last.astype(F32)  1.66 us

profile of v9, /device:TPU:0, one launch (start us, length us, event | category | flops | bytes accessed | tf_op | source)
XLA Modules:
  0.0 58.1 jit_solution(1117929536303562858)
XLA Ops:
  0.7 0.0 copy-start
  0.7 0.7 %copy-done = f32[32,32]{1,0:T(8,128)S(1)} copy-done((f32[32,32]{1,0:T(8,128)S(1)}, f32[32,32]{1,0:T(8,128)}, u32[]{:S(2)}) %copy-start) | copy-done | bytes 4120
  1.4 55.1 %shard_map.55 = (f32[1024,512]{1,0:T(8,128)S(1)}, bf16[1024,512]{1,0:T(8,128)(2,1)S(1)}) custom-call(f32[1024,512]{1,0:T(8,128)} %bitcast.9, f32[1024,512]{1,0:T(8,128)} %bitcast.10, f32[32,32]{1,0:T(8,128)S(1)} %copy-done, bf16[1600,1024]{1,0:T(8,128)(2,1)} %bitcast.8, f32[1]{0:T(128)} %bitcast.7.om_ref), custom_call_target="tpu_custom_call" | custom-call | tf_op jit(solution)/shard_map/pallas_call | solution.py:534
  56.5 1.7 %multiply_add_fusion = f32[1024,512]{1,0:T(8,128)} fusion(f32[1024,512]{1,0:T(8,128)S(1)} %get-tuple-element.7, bf16[1024,512]{1,0:T(8,128)(2,1)S(1)} %get-tuple-element.8, f32[]{:T(128)} %copy.6), kind=kLoop, calls=%fused_computation | loop fusion | flops 1572864 | bytes 5242884 | tf_op jit(solution)/shard_map/add | solution.py:582
Async XLA Ops:
  0.7 0.7 %copy-start = (f32[32,32]{1,0:T(8,128)S(1)}, f32[32,32]{1,0:T(8,128)}, u32[]{:S(2)}) copy-start(f32[32,32]{1,0:T(8,128)} %kap_ref.1) | copy-start | bytes 12292

commit v10 on v9

--- a/solution.py
+++ b/solution.py
@@ -252,7 +252,7 @@
             @pl.when(jnp.logical_and(turn, detour[s]))
             def _():
                 for i in which:
-                    message_out(g, s, t, i).start()
+                    (message if i == 0 else message_out)(g, s, t, i).start()
 
     def fwd_rows(g):
         rows = pl.multiple_of((SUB - MARGIN) * SUB * (1 - row), 128)
@@ -301,23 +301,25 @@
     def assemble_far(g, sent, first):
         assemble(g, sent, first, far, (4, 3))
 
-    def pack(g, scaled):
+    def pack(g):
         def one_row(q, carry):
             rows = pl.ds(pl.multiple_of(q * SUB, SUB), SUB)
             for t in range(TILES):
                 k = g * TILES + t
                 e_v[g, rows, pl.ds(t * LANES, LANES)] = (keep * res[k, rows]).astype(BF16)
-                z = zf[k, pl.ds(pl.multiple_of(PAD + q * SUB, PAD), SUB)]
-                u_v[k, rows] = u_v[k, rows] + om * z if scaled else z
             return carry
 
         lax.fori_loop(0, SUB, one_row, 0, unroll=4)
         fwd_rows(g).start()
 
-    def solve_own(g):
+    def solve_own(g, scaled):
         def rows_of(m, carry):
             rows = pl.ds(pl.multiple_of(m * (CELLS // 2), CELLS // 2), CELLS // 2)
             acc[g, rows] = jnp.dot(mat_p[rows, :COLS_AT], e_v[g, pl.ds(0, COLS_AT)], preferred_element_type=F32)
+            for t in range(TILES):
+                k = g * TILES + t
+                z = zf[k, pl.ds(pl.multiple_of(PAD + m * (CELLS // 2), PAD), CELLS // 2)]
+                u_v[k, rows] = u_v[k, rows] + om * z if scaled else z
             return carry
 
         lax.fori_loop(0, 2, rows_of, 0)
@@ -383,8 +385,8 @@
         send_bands(g, 0, 0)
 
     def finish(g, scaled):
-        pack(g, scaled)
-        solve_own(g)
+        pack(g)
+        solve_own(g, scaled)
 
     mat_copy.wait()
     for at in range(0, EXT * EXT, 256):
@@ -458,11 +460,12 @@
         @pl.when(is_via)
         def _():
             for i in which:
-                message_on(g, 0, i).wait_send()
+                if i != 0:
+                    message_on(g, 0, i).wait_send()
 
     def advance(g, t, first, relay):
         if relay is not None:
-            pass_on(relay[0], relay[1], (0, 2, 1))
+            pass_on(relay[0], relay[1], (2, 1))
         solve_rest(g)
         round_row(g)
         zrow_copy(g).start()
@@ -509,7 +512,7 @@
                 u_copies[TILES + t].start()
         assemble_far(g, SWEEPS - 1, False)
         if g == 0:
-            pass_on(1, SWEEPS - 1, (0, 2, 1))
+            pass_on(1, SWEEPS - 1, (2, 1))
         solve_rest(g)
         z_v[g] = acc[g].astype(BF16)
         z_copies[g].start()

time: 58.3 us -> 58.3 us (level)
  no operation moved by 1% of the time
where the time goes in v10:
time: 58.3 us; the launch traced here: 58.1 us
  Pallas kernels  55 us (94%)
  other arithmetic  1.66 us (3%)
  local copies, waits for them, and re-layouts  0.71 us (1%)
  between operations  0.67 us (1%)
    pallas_call x1, Pallas kernels, device_fn(): pl.pallas_call(functools.partial(kernel, groups, col_count), out_shape=(j...  55 us
    add x1, other arithmetic, device_fn(): u_last + omega_relax * z_last.astype(F32)  1.66 us

profile of v10, /device:TPU:0, one launch (start us, length us, event | category | flops | bytes accessed | tf_op | source)
XLA Modules:
  0.0 58.1 jit_solution(9585008566289431186)
XLA Ops:
  0.7 0.0 copy-start
  0.7 0.7 %copy-done = f32[32,32]{1,0:T(8,128)S(1)} copy-done((f32[32,32]{1,0:T(8,128)S(1)}, f32[32,32]{1,0:T(8,128)}, u32[]{:S(2)}) %copy-start) | copy-done | bytes 4120
  1.4 55.0 %shard_map.55 = (f32[1024,512]{1,0:T(8,128)S(1)}, bf16[1024,512]{1,0:T(8,128)(2,1)S(1)}) custom-call(f32[1024,512]{1,0:T(8,128)} %bitcast.9, f32[1024,512]{1,0:T(8,128)} %bitcast.10, f32[32,32]{1,0:T(8,128)S(1)} %copy-done, bf16[1600,1024]{1,0:T(8,128)(2,1)} %bitcast.8, f32[1]{0:T(128)} %bitcast.7.om_ref), custom_call_target="tpu_custom_call" | custom-call | tf_op jit(solution)/shard_map/pallas_call | solution.py:537
  56.4 1.7 %multiply_add_fusion = f32[1024,512]{1,0:T(8,128)} fusion(f32[1024,512]{1,0:T(8,128)S(1)} %get-tuple-element.7, bf16[1024,512]{1,0:T(8,128)(2,1)S(1)} %get-tuple-element.8, f32[]{:T(128)} %copy.6), kind=kLoop, calls=%fused_computation | loop fusion | flops 1572864 | bytes 5242884 | tf_op jit(solution)/shard_map/add | solution.py:585
Async XLA Ops:
  0.7 0.7 %copy-start = (f32[32,32]{1,0:T(8,128)S(1)}, f32[32,32]{1,0:T(8,128)}, u32[]{:S(2)}) copy-start(f32[32,32]{1,0:T(8,128)} %kap_ref.1) | copy-start | bytes 12292
